TPU v7x, 256 devices: a whole 4x4x8 slice. The times are simulated.
256 devices in a mesh: grp: 4 (over x), mem: 64 (over z, y, core).
Axes of the slice: x: 4, y: 4, z: 8, core: 2. Of those that a mesh axis runs over, the one named last changes fastest.
Arguments:
- background_tensor: bfloat16 [512, 256, 1024], P('grp', 'mem'), may hold values from -6 to 6
- reading_tally: int32 [512], P(('grp', 'mem')), may hold values from 128 to 1024, as said below
- measurement_slot: int32 [512, 1024], P(('grp', 'mem')), may hold values from 0 to 1023
- reading_datum: float32 [512, 1024], P(('grp', 'mem')), may hold values from -6 to 6
- error_precision: float32 [512, 1024], P(('grp', 'mem')), may hold values from 0.5 to 16
- reading_offset: float32 [512, 1024], P(('grp', 'mem')), may hold values from 0 to 1
Outputs:
- analysis: bfloat16 [512, 256, 1024], P('grp', 'mem')
Inputs may be any that keep to these rules, and one draw needn't show every extreme that they name: `reading_tally`: each column's live observations fill its first slots; at least one column has exactly 1024.
All inputs are finite; a program needn't handle non-finite values.
Results may differ from a plain program's by a relative error of at most 0.0074.
Values may be sent and summed in bfloat16 or wider, within the bound.
No kernel may reach another device: no remote copies, remote signals or barrier semaphores. Data moves between devices by JAX's collectives and lax.ppermute only.
A program may use at most 64 MiB of HBM per device.

v0:
```python
import jax
import jax.numpy as jnp
from jax import lax
from jax.sharding import PartitionSpec as P

NSTEPS = 5


def extended(value, sides, width):
    edges = {}
    for axis, dim in sides:
        count, length = (lax.axis_size(axis), value.shape[dim])
        up = [(i, (i + 1) % count) for i in range(count)]
        last = lax.slice_in_dim(value, length - width, length, axis=dim)
        leading = lax.slice_in_dim(value, 0, width, axis=dim)
        edges[dim] = (
            lax.ppermute(last, axis, up),
            lax.ppermute(leading, axis, [(b, a) for a, b in up]),
        )
    done = []
    for _, dim in sides:
        low, high = edges[dim]
        around = [(width, width) if d in done else (0, 0) for d in range(value.ndim)]
        value = jnp.concatenate([jnp.pad(low, around), value, jnp.pad(high, around)], axis=dim)
        done.append(dim)
    return value


def direction_weights(shift_amount):
    toward_west = jnp.exp(-((shift_amount + 0.5) ** 2))
    own_weight = jnp.exp(-((shift_amount - 0.5) ** 2))
    toward_east = jnp.exp(-((1.5 - shift_amount) ** 2))
    return (toward_west, own_weight, toward_east)


def dense_grams(obs_rows, sample_slices):
    return jnp.einsum(
        "ekm,ejm->ekj", obs_rows, obs_rows[:, :sample_slices], preferred_element_type=jnp.float32
    )


def grams(obs_rows, sample_slices):
    return dense_grams(obs_rows, sample_slices)


def per_device(
    background_tensor,
    reading_tally,
    measurement_slot,
    reading_datum,
    error_precision,
    reading_offset,
):
    background_members = lax.all_to_all(
        background_tensor, "mem", split_axis=0, concat_axis=1, tiled=True
    )
    vertical_slices, sample_slices, vertical_numbers = background_members.shape
    obs_slots = measurement_slot.shape[1]
    model_vector32 = background_members.astype(jnp.float32)
    focal_site = jnp.sum(model_vector32, axis=1) / sample_slices
    anomaly_matrix = (model_vector32 - focal_site[:, None, :]).astype(jnp.bfloat16)
    measured_vector = jax.vmap(lambda source, picks: jnp.take(source, picks, axis=1))(
        anomaly_matrix, measurement_slot
    )
    seen_mean = jax.vmap(lambda source, picks: jnp.take(source, picks, axis=0))(
        focal_site, measurement_slot
    )
    innovation = reading_datum - seen_mean
    live_mask = (jnp.arange(obs_slots, dtype=jnp.int32)[None, :] < reading_tally[:, None]).astype(
        jnp.float32
    )
    toward_west, own_weight, toward_east = direction_weights(reading_offset)

    def rows_with(weight):
        factor = jnp.sqrt(weight * error_precision) * live_mask
        scaled = (measured_vector.astype(jnp.float32) * factor[:, None, :]).astype(jnp.bfloat16)
        shifted = (innovation * factor).astype(jnp.bfloat16)
        padding = jnp.zeros((vertical_slices, 7, obs_slots), jnp.bfloat16)
        return jnp.concatenate([scaled, shifted[:, None, :], padding], axis=1)

    own_rows = rows_with(own_weight)
    side_rows = jnp.stack([rows_with(toward_west), rows_with(toward_east)], axis=1)
    side_rows = side_rows.reshape(2 * vertical_slices, sample_slices + 8, obs_slots)
    own_gram = grams(own_rows, sample_slices)
    side_gram = grams(side_rows, sample_slices)
    widened = extended(side_gram, ((("grp", "mem"), 0),), 1)
    combined = (
        own_gram + widened[0 : 2 * vertical_slices : 2] + widened[3 : 2 * vertical_slices + 2 : 2]
    )
    identity = jnp.eye(sample_slices, dtype=jnp.float32)
    system = (sample_slices - 1) * identity[None] + combined[:, :sample_slices]
    pull_vec = combined[:, sample_slices]
    norm_value = jnp.sqrt(jnp.sum(system * system, axis=(1, 2)))
    iterate = system / norm_value[:, None, None]
    inverse = jnp.broadcast_to(identity, system.shape)
    for iteration in range(NSTEPS):
        middle = 1.5 * identity[None] - 0.5 * jnp.einsum(
            "cij,cjk->cik", inverse, iterate, precision=lax.Precision.HIGHEST
        )
        iterate = jnp.einsum("cij,cjk->cik", iterate, middle, precision=lax.Precision.HIGHEST)
        inverse = jnp.einsum("cij,cjk->cik", middle, inverse, precision=lax.Precision.HIGHEST)
    inv_root = inverse / jnp.sqrt(norm_value)[:, None, None]
    inner = jnp.einsum("cij,cj->ci", inv_root, pull_vec, precision=lax.Precision.HIGHEST)
    mean_weight = jnp.einsum("cij,cj->ci", inv_root, inner, precision=lax.Precision.HIGHEST)
    weight_matrix = (jnp.sqrt(sample_slices - 1.0) * inv_root + mean_weight[:, :, None]).astype(
        jnp.bfloat16
    )
    increment = jnp.einsum(
        "mar,mao->mro", weight_matrix, anomaly_matrix, preferred_element_type=jnp.float32
    )
    analysis = (focal_site[:, None, :] + increment).astype(jnp.bfloat16)
    return lax.all_to_all(analysis, "mem", split_axis=1, concat_axis=0, tiled=True)


def solution(mesh):
    in_specs = (
        P("grp", "mem", None),
        P(("grp", "mem")),
        P(("grp", "mem"), None),
        P(("grp", "mem"), None),
        P(("grp", "mem"), None),
        P(("grp", "mem"), None),
    )
    out_specs = P("grp", "mem", None)
    return jax.shard_map(
        per_device, mesh=mesh, in_specs=in_specs, out_specs=out_specs, check_vma=False
    )
```

profile of v0, /device:TPU:1, one launch (start us, length us, event | category | flops | bytes accessed | tf_op | source)
XLA Modules:
  0.0 142.4 jit_solution(5990883633996563869)
XLA Ops:
  0.0 13.3 %all-to-all-start = ((bf16[128,4,1024]{2,1,0:T(4,128)(2,1)}), bf16[128,4,1024]{2,1,0:T(4,128)(2,1)S(1)}, u32[]{:S(2)}, u32[]{:S(2)}) async-start(bf16[128,4,1024]{2,1,0:T(4,128)(2,1)} %param.6), calls=%async_computation | async-start | bytes 2097152 | tf_op jit(solution)/shard_map/all_to_all | solution.py:54
  13.3 0.1 pad.13.clone
  13.4 28.0 %all-to-all-done = bf16[128,4,1024]{2,1,0:T(4,128)(2,1)S(1)} async-done(((bf16[128,4,1024]{2,1,0:T(4,128)(2,1)}), bf16[128,4,1024]{2,1,0:T(4,128)(2,1)S(1)}, u32[]{:S(2)}, u32[]{:S(2)}) %all-to-all-start) | async-done | bytes 1048608 | tf_op jit(solution)/shard_map/all_to_all | solution.py:54
  41.5 1.4 convert_reduce_fusion
  42.9 0.3 reduce_sum.26
  43.2 0.2 reduce_sum.27
  43.4 0.0 copy-start.1
  43.4 0.0 copy-start.3
  43.4 17.7 %gather_fusion.1 = f32[2048]{0:T(1024)S(1)} fusion(f32[2,1024]{1,0:T(2,128)S(1)} %broadcast_multiply_fusion, s32[2048]{0:T(1024)S(1)} %bitcast.74), kind=kCustom, calls=%fused_computation.1 | custom fusion | bytes 32768 | tf_op jit(solution)/shard_map/vmap(jit(_take))/gather | solution.py:65
  61.2 0.1 fusion.35
  61.3 0.1 fusion.36
  61.3 0.6 copy_bitcast_fusion
  62.0 1.8 %reshape.44 = f32[2,256,1024]{2,1,0:T(8,128)} reshape(f32[2,64,4,1024]{3,2,1,0:T(4,128)S(1)} %copy_bitcast_fusion) | data formatting | bytes 4194304 | tf_op jit(solution)/shard_map/convert_element_type | solution.py:59
  63.7 1.8 %subtract_convert_fusion = bf16[2,256,1024]{2,1,0:T(8,128)(2,1)S(1)} fusion(f32[2,256,1024]{2,1,0:T(8,128)} %reshape.44, f32[2,1024]{1,0:T(2,128)S(1)} %broadcast_multiply_fusion), kind=kLoop, calls=%fused_computation.13 | loop fusion | flops 1048576 | bytes 3153920 | tf_op jit(solution)/shard_map/convert_element_type | solution.py:61
  65.6 0.5 copy.66
  66.1 11.1 %gather_fusion = bf16[2048,256]{1,0:T(8,128)(2,1)S(1)} fusion(bf16[2,256,1024]{1,2,0:T(8,128)(2,1)S(1)} %copy.66, s32[2048]{0:T(1024)S(1)} %bitcast.75), kind=kCustom, calls=%fused_computation | custom fusion | bytes 2113536 | tf_op jit(solution)/shard_map/vmap(jit(_take))/gather | solution.py:62
  77.2 0.5 copy.67
  77.8 0.7 fusion.18
  78.5 0.7 maximum_bitcast_fusion
  79.2 0.2 pad_maximum_fusion
  79.4 0.2 copy.72
  79.6 0.9 fusion.3
  80.6 2.3 %collective-permute-start = (f32[1,264,256]{2,1,0:T(8,128)S(1)}, f32[1,264,256]{2,1,0:T(8,128)S(1)}, u32[]{:S(2)}, u32[]{:S(2)}) collective-permute-start(f32[1,264,256]{2,1,0:T(8,128)S(1)} %get-tuple-element.13), channel_id=1, source_target_pairs={{0,1},{1,2},{2,3},{3,4},{4,5},{5,6},{6,7},{7,8},{8,9},{9,10},{10,1... | collective-permute-start | bytes 811016 | tf_op jit(solution)/shard_map/ppermute | solution.py:17
  83.0 3.3 %collective-permute-done = f32[1,264,256]{2,1,0:T(8,128)S(1)} collective-permute-done((f32[1,264,256]{2,1,0:T(8,128)S(1)}, f32[1,264,256]{2,1,0:T(8,128)S(1)}, u32[]{:S(2)}, u32[]{:S(2)}) %collective-permute-start) | collective-permute-done | bytes 270368 | tf_op jit(solution)/shard_map/ppermute | solution.py:17
  86.3 2.5 %collective-permute-done.1 = f32[1,264,256]{2,1,0:T(8,128)S(1)} collective-permute-done((f32[1,264,256]{2,1,0:T(8,128)S(1)}, f32[1,264,256]{2,1,0:T(8,128)S(1)}, u32[]{:S(2)}, u32[]{:S(2)}) %collective-permute-start.1) | collective-permute-done | bytes 270368 | tf_op jit(solution)/shard_map/ppermute | solution.py:18
  88.8 0.1 pad_maximum_fusion.1
  88.9 0.7 slice_add_fusion
  89.6 0.2 multiply_reduce_fusion
  89.8 0.7 fusion.9
  90.5 0.7 fusion.44
  91.2 0.6 fusion.28
  91.9 0.7 fusion.8
  92.5 0.7 fusion.49
  93.2 0.7 fusion.48
  93.9 0.7 fusion.7
  94.5 0.7 fusion.51
  95.2 0.7 fusion.50
  95.9 0.7 fusion.6
  96.6 0.7 fusion.53
  97.2 0.7 fusion.52
  97.9 0.7 fusion.5
  98.6 0.7 convolution_divide_fusion
  99.2 0.5 fusion.38
  99.8 0.6 fusion.39
  100.3 0.6 add_convert_fusion
  100.9 1.1 copy.74
  102.0 38.9 %all_to_all.27 = bf16[2,256,1024]{2,0,1:T(2,128)(2,1)S(1)} all-to-all(bf16[2,256,1024]{2,0,1:T(2,128)(2,1)S(1)} %copy.74), channel_id=1, replica_groups=mesh['grp'=4,'mem'=64] {'mem'}, dimensions={1} | all-to-all | bytes 2097152 | tf_op jit(solution)/shard_map/all_to_all | solution.py:112
  140.9 1.5 %copy.75 = bf16[64,2,4,1024]{3,2,1,0:T(4,128)(2,1)} copy(bf16[64,2,4,1024]{3,1,2,0:T(2,128)(2,1)S(1)} %bitcast.78) | data formatting | bytes 2097152 | tf_op jit(solution)/shard_map/all_to_all | solution.py:112
  (23 shorter events, 0.2 us)
Async XLA Ops:
  0.0 13.3 %copy-start.2 = (s32[2,1024]{1,0:T(2,128)S(1)}, s32[2,1024]{1,0:T(2,128)}, u32[]{:S(2)}) copy-start(s32[2,1024]{1,0:T(2,128)} %param.8) | copy-start | bytes 24580
  0.0 41.5 %all-to-all-start = ((bf16[128,4,1024]{2,1,0:T(4,128)(2,1)}), bf16[128,4,1024]{2,1,0:T(4,128)(2,1)S(1)}, u32[]{:S(2)}, u32[]{:S(2)}) async-start(bf16[128,4,1024]{2,1,0:T(4,128)(2,1)} %param.6), calls=%async_computation | async-start | bytes 2097152 | tf_op jit(solution)/shard_map/all_to_all | solution.py:54
  43.4 17.7 %copy-start = (f32[2,1024]{1,0:T(2,128)S(1)}, f32[2,1024]{1,0:T(2,128)}, u32[]{:S(2)}) copy-start(f32[2,1024]{1,0:T(2,128)} %param.10) | copy-start | bytes 24580
  43.4 17.8 %copy-start.1 = (f32[2,1024]{1,0:T(2,128)S(1)}, f32[2,1024]{1,0:T(2,128)}, u32[]{:S(2)}) copy-start(f32[2,1024]{1,0:T(2,128)} %param.11) | copy-start | bytes 24580
  43.4 17.7 %copy-start.3 = (f32[2,1024]{1,0:T(2,128)S(1)}, f32[2,1024]{1,0:T(2,128)}, u32[]{:S(2)}) copy-start(f32[2,1024]{1,0:T(2,128)} %param.9) | copy-start | bytes 24580
  43.4 17.7 %copy-start.4 = (s32[2]{0:T(128)S(1)}, s32[2]{0:T(128)}, u32[]{:S(2)}) copy-start(s32[2]{0:T(128)} %param.7) | copy-start | bytes 28
  80.6 5.7 %collective-permute-start = (f32[1,264,256]{2,1,0:T(8,128)S(1)}, f32[1,264,256]{2,1,0:T(8,128)S(1)}, u32[]{:S(2)}, u32[]{:S(2)}) collective-permute-start(f32[1,264,256]{2,1,0:T(8,128)S(1)} %get-tuple-element.13), channel_id=1, source_target_pairs={{0,1},{1,2},{2,3},{3,4},{4,5},{5,6},{6,7},{7,8},{8,9},{9,10},{10,1... | collective-permute-start | bytes 811016 | tf_op jit(solution)/shard_map/ppermute | solution.py:17
  82.9 5.9 %collective-permute-start.1 = (f32[1,264,256]{2,1,0:T(8,128)S(1)}, f32[1,264,256]{2,1,0:T(8,128)S(1)}, u32[]{:S(2)}, u32[]{:S(2)}) collective-permute-start(f32[1,264,256]{2,1,0:T(8,128)S(1)} %get-tuple-element.14), channel_id=1, source_target_pairs={{1,0},{2,1},{3,2},{4,3},{5,4},{6,5},{7,6},{8,7},{9,8},{10,9},{11,1... | collective-permute-start | bytes 811016 | tf_op jit(solution)/shard_map/ppermute | solution.py:18
where the time goes:
time: 143 us; the launch traced here: 142 us
  blocking collectives  38.9 us (27%)
  local copies, waits for them, and re-layouts  34.9 us (24%)
  waiting for transfers between devices  33.8 us (24%)
  starting transfers between devices  15.6 us (11%)
  matrix products  12.5 us (9%)
  other arithmetic  6.26 us (4%)
    all_to_all x1, blocking collectives, per_device(): lax.all_to_all(analysis, 'mem', split_axis=1, concat_axis=0, tiled=True)  38.9 us
    all_to_all x1, waiting for transfers between devices, per_device(): lax.all_to_all(background_tensor, 'mem', split_axis=0, concat_axis=1, til...  28 us
    gather x2, local copies, waits for them, and re-layouts, per_device(): jnp.take(source, picks, axis=0)  17.7 us
    all_to_all x1, starting transfers between devices, per_device(): lax.all_to_all(background_tensor, 'mem', split_axis=0, concat_axis=1, til...  13.3 us
    gather x2, local copies, waits for them, and re-layouts, per_device(): jnp.take(source, picks, axis=1)  11.6 us
    dot_general x5, matrix products, per_device(): jnp.einsum('cij,cjk->cik', inverse, iterate, precision=lax.Precision.HIGH...  3.38 us
    ppermute x1, waiting for transfers between devices, extended(): lax.ppermute(last, axis, up)  3.32 us
    dot_general x5, matrix products, per_device(): jnp.einsum('cij,cjk->cik', middle, inverse, precision=lax.Precision.HIGHEST)  3.27 us
  transfers between devices with their start and end apart: 3, of which 3 were waited for; matrix products, arithmetic and copies ran while one was open for 0% of the time, Pallas kernels for 0%

commit v1 on v0

v1 whole, which is shorter than its diff:
```python
import jax
import jax.numpy as jnp
from jax import lax
from jax.sharding import PartitionSpec as P

NSTEPS = 5
HIGH = lax.Precision.HIGH
HIGHEST = lax.Precision.HIGHEST


def direction_weights(shift_amount):
    toward_west = jnp.exp(-((shift_amount + 0.5) ** 2))
    own_weight = jnp.exp(-((shift_amount - 0.5) ** 2))
    toward_east = jnp.exp(-((1.5 - shift_amount) ** 2))
    return (toward_west, own_weight, toward_east)


def binned(tally, slot, datum, precision, offset, values):
    slots = slot.shape[0]
    live = (jnp.arange(slots, dtype=jnp.int32) < tally).astype(jnp.float32)
    weights = jnp.stack(direction_weights(offset)) * (precision * live)[None]
    rows = jnp.concatenate([weights, weights * datum[None]], axis=0)
    chosen = (slot[:, None] == jnp.arange(values, dtype=jnp.int32)[None, :]).astype(jnp.float32)
    return jnp.dot(rows, chosen, precision=HIGHEST)


def summary(members):
    wide = members.astype(jnp.float32)
    center = jnp.sum(wide, axis=0) / members.shape[0]
    return center, (wide - center[None]).astype(jnp.bfloat16)


def products(center, spread, bins, which):
    weight, driven = bins[which], bins[3 + which]
    rows = (spread.astype(jnp.float32) * jnp.sqrt(weight)[None]).astype(jnp.bfloat16)
    gram = lax.dot_general(
        rows, rows, (((1,), (1,)), ((), ())), preferred_element_type=jnp.float32
    )
    drive = driven - weight * center
    pull = lax.dot_general(
        jnp.broadcast_to(drive[None], (8, drive.shape[0])),
        spread.astype(jnp.float32),
        (((1,), (1,)), ((), ())),
        precision=HIGH,
    )
    return jnp.concatenate([gram, pull], axis=0)


def transform_of(combined):
    count = combined.shape[1]
    eye = jnp.eye(count, dtype=jnp.float32)
    system = (count - 1) * eye + combined[:count]
    pull = combined[count]
    norm = jnp.sqrt(jnp.sum(system * system))
    iterate = system / norm
    inverse = 1.5 * eye - 0.5 * iterate
    iterate = jnp.dot(iterate, inverse, precision=HIGH)
    for step in range(1, NSTEPS):
        middle = 1.5 * eye - 0.5 * jnp.dot(inverse, iterate, precision=HIGH)
        if step < NSTEPS - 1:
            iterate = jnp.dot(iterate, middle, precision=HIGH)
        inverse = jnp.dot(middle, inverse, precision=HIGH)
    root = inverse / jnp.sqrt(norm)
    inner = jnp.dot(root, pull, precision=HIGHEST)
    mean_weight = jnp.dot(root, inner, precision=HIGHEST)
    return (jnp.sqrt(count - 1.0) * root + mean_weight[:, None]).astype(jnp.bfloat16)


def analysed(center, spread, transform):
    grown = lax.dot_general(
        transform, spread, (((0,), (0,)), ((), ())), preferred_element_type=jnp.float32
    )
    return (center[None] + grown).astype(jnp.bfloat16)


def exchange(value):
    return lax.all_to_all(value, "mem", split_axis=0, concat_axis=0, tiled=True)


def per_device(background, tally, slot, datum, precision, offset):
    columns, held, values = background.shape
    sides = background.reshape(columns // 2, 2, held, values)
    even_in = exchange(sides[:, 0])
    odd_in = exchange(sides[:, 1])
    bins = [
        binned(tally[c], slot[c], datum[c], precision[c], offset[c], values) for c in range(2)
    ]
    count = lax.axis_size("grp") * lax.axis_size("mem")
    up = [(i, (i + 1) % count) for i in range(count)]
    down = [(b, a) for a, b in up]
    even_in = even_in.reshape(-1, values)
    odd_in = odd_in.reshape(-1, values)
    even_center, even_spread = summary(even_in)
    from_east = lax.ppermute(products(even_center, even_spread, bins[0], 0), ("grp", "mem"), down)
    even_own = products(even_center, even_spread, bins[0], 1)
    even_east = products(even_center, even_spread, bins[0], 2)

    odd_center, odd_spread = summary(odd_in)
    from_west = lax.ppermute(products(odd_center, odd_spread, bins[1], 2), ("grp", "mem"), up)
    odd_own = products(odd_center, odd_spread, bins[1], 1)
    odd_west = products(odd_center, odd_spread, bins[1], 0)

    odd_out = analysed(odd_center, odd_spread, transform_of(odd_own + even_east + from_east))
    odd_out = exchange(odd_out.reshape(columns // 2, held, values))
    even_out = analysed(even_center, even_spread, transform_of(even_own + from_west + odd_west))
    even_out = exchange(even_out.reshape(columns // 2, held, values))
    return jnp.stack([even_out, odd_out], axis=1).reshape(columns, held, values)


def solution(mesh):
    both = ("grp", "mem")
    in_specs = (
        P("grp", "mem", None),
        P(both),
        P(both, None),
        P(both, None),
        P(both, None),
        P(both, None),
    )
    return jax.shard_map(
        per_device, mesh=mesh, in_specs=in_specs, out_specs=P("grp", "mem", None), check_vma=False
    )
```

time: 143 us -> 137 us (0.958)
  local copies, waits for them, and re-layouts: 34.9 us -> 7.28 us
  blocking collectives: 38.9 us -> 23.2 us
  starting transfers between devices: 15.6 us -> 31.1 us
  waiting for transfers between devices: 33.8 us -> 46.1 us
  matrix products: 12.5 us -> 17.5 us
  other arithmetic: 6.26 us -> 8.95 us
  between operations: 0.4 us -> 2.01 us
    gather x4 -> x0, local copies, waits for them, and re-layouts: 29.3 us -> none  [the longest x2 17.7 us: per_device(): jnp.take(source, picks, axis=0)]
    all_to_all x1 -> x3, waiting for transfers between devices: 28 us -> 46.1 us  [exchange(): return lax.all_to_all(value, 'mem', split_axis=0, concat_axis=0, tiled=True)]
    all_to_all x1 -> x3, starting transfers between devices: 13.3 us -> 29.6 us  [exchange(): return lax.all_to_all(value, 'mem', split_axis=0, concat_axis=0, tiled=True)]
    all_to_all x1, blocking collectives: 38.9 us -> 23.2 us  [exchange(): return lax.all_to_all(value, 'mem', split_axis=0, concat_axis=0, tiled=True)]
    ppermute x2, waiting for transfers between devices: 5.8 us -> 0.01 us  [the longest x1 0.01 us: per_device(): lax.ppermute(products(even_center, even_spread, bins[0], 0), ('grp', 'mem...]
    dot_general x19 -> x44, matrix products: 12.5 us -> 17.5 us  [the longest x6 3.45 us: products(): lax.dot_general(rows, rows, (((1,), (1,)), ((), ())), preferred_element_t...]
    convert_element_type x3 -> x8, local copies, waits for them, and re-layouts: 3.39 us -> 0.86 us  [the longest x6 0.72 us: products(): (spread.astype(jnp.float32) * jnp.sqrt(weight)[None]).astype(jnp.bfloat16)]
    squeeze x0 -> x1, local copies, waits for them, and re-layouts: none -> 2.52 us  [per_device(): even_in = exchange(sides[:, 0])]
  transfers between devices with their start and end apart: 3 -> 5, of which waited for: 3 -> 3; matrix products, arithmetic and copies ran while one was open for 0% -> 12% of each run, Pallas kernels for 0% -> 0%
where the time goes in v1:
time: 137 us; the launch traced here: 136 us
  waiting for transfers between devices  46.1 us (34%)
  starting transfers between devices  31.1 us (23%)
  blocking collectives  23.2 us (17%)
  matrix products  17.5 us (13%)
  other arithmetic  8.95 us (7%)
  local copies, waits for them, and re-layouts  7.28 us (5%)
  between operations  2.01 us (1%)
    all_to_all x3, waiting for transfers between devices, exchange(): return lax.all_to_all(value, 'mem', split_axis=0, concat_axis=0, tiled=True)  46.1 us
    all_to_all x3, starting transfers between devices, exchange(): return lax.all_to_all(value, 'mem', split_axis=0, concat_axis=0, tiled=True)  29.6 us
    all_to_all x1, blocking collectives, exchange(): return lax.all_to_all(value, 'mem', split_axis=0, concat_axis=0, tiled=True)  23.2 us
    dot_general x6, matrix products, products(): lax.dot_general(rows, rows, (((1,), (1,)), ((), ())), preferred_element_t...  3.45 us
    dot_general x2, matrix products, binned(): return jnp.dot(rows, chosen, precision=HIGHEST)  2.93 us
  transfers between devices with their start and end apart: 5, of which 3 were waited for; matrix products, arithmetic and copies ran while one was open for 12% of the time, Pallas kernels for 0%

profile of v1, /device:TPU:1, one launch (start us, length us, event | category | flops | bytes accessed | tf_op | source)
XLA Modules:
  0.0 136.1 jit_solution(11457862928314036056)
XLA Ops:
  0.0 2.5 %slice_bitcast_fusion.1 = (bf16[64,4,1024]{2,1,0:T(4,128)(2,1)}, bf16[64,4,1024]{2,1,0:T(4,128)(2,1)}) fusion(bf16[64,2,4,1024]{3,2,1,0:T(4,128)(2,1)} %bitcast.118), kind=kLoop, calls=%fused_computation.50 | loop fusion | bytes 2097152 | tf_op jit(solution)/shard_map/squeeze | solution.py:83
  2.6 13.3 %all-to-all-start = ((bf16[64,4,1024]{2,1,0:T(4,128)(2,1)}), bf16[64,4,1024]{2,1,0:T(4,128)(2,1)S(1)}, u32[]{:S(2)}, u32[]{:S(2)}) async-start(bf16[64,4,1024]{2,1,0:T(4,128)(2,1)} %get-tuple-element.5), calls=%async_computation | async-start | bytes 1048576 | tf_op jit(solution)/shard_map/all_to_all | solution.py:77
  15.9 0.6 fusion.98
  16.5 1.2 compare_select_fusion
  17.8 15.8 %all-to-all-done = bf16[64,4,1024]{2,1,0:T(4,128)(2,1)S(1)} async-done(((bf16[64,4,1024]{2,1,0:T(4,128)(2,1)}), bf16[64,4,1024]{2,1,0:T(4,128)(2,1)S(1)}, u32[]{:S(2)}, u32[]{:S(2)}) %all-to-all-start) | async-done | bytes 524320 | tf_op jit(solution)/shard_map/all_to_all | solution.py:77
  33.5 5.7 %all-to-all-start.1 = ((bf16[64,4,1024]{2,1,0:T(4,128)(2,1)}), bf16[64,4,1024]{2,1,0:T(4,128)(2,1)S(1)}, u32[]{:S(2)}, u32[]{:S(2)}) async-start(bf16[64,4,1024]{2,1,0:T(4,128)(2,1)} %get-tuple-element.6), calls=%async_computation.1 | async-start | bytes 1048576 | tf_op jit(solution)/shard_map/all_to_all | solution.py:77
  39.3 1.5 %fusion = f32[6,1024]{1,0:T(8,128)S(1)} fusion(s32[1024]{0:T(1024)S(1)} %bitcast.138, f32[3,1024]{1,0:T(4,128)S(1)} %get-tuple-element.34, f32[3,1024]{1,0:T(4,128)S(1)} %get-tuple-element.33), kind=kOutput, calls=%fused_computation.2 | convolution fusion | flops 76552192 | bytes 53248 | tf_op jit(solution)/shard_map/dot_general | solution.py:24
  40.7 1.5 %fusion.1 = f32[6,1024]{1,0:T(8,128)S(1)} fusion(s32[1024]{0:T(1024)S(1)} %bitcast.137, f32[3,1024]{1,0:T(4,128)S(1)} %get-tuple-element.49, f32[3,1024]{1,0:T(4,128)S(1)} %get-tuple-element.50), kind=kOutput, calls=%fused_computation.3 | convolution fusion | flops 76552192 | bytes 53248 | tf_op jit(solution)/shard_map/dot_general | solution.py:24
  42.4 14.5 %all-to-all-done.1 = bf16[64,4,1024]{2,1,0:T(4,128)(2,1)S(1)} async-done(((bf16[64,4,1024]{2,1,0:T(4,128)(2,1)}), bf16[64,4,1024]{2,1,0:T(4,128)(2,1)S(1)}, u32[]{:S(2)}, u32[]{:S(2)}) %all-to-all-start.1) | async-done | bytes 524320 | tf_op jit(solution)/shard_map/all_to_all | solution.py:77
  57.4 0.4 fusion.60
  57.8 0.4 fusion.62
  58.1 0.4 fusion.64
  58.5 0.6 fusion.18
  59.3 1.1 fusion.101
  60.5 0.3 fusion.108
  61.0 0.3 fusion.100
  61.3 0.7 pad_maximum_fusion.1
  62.0 1.5 %collective-permute-start = (f32[264,256]{1,0:T(8,128)}, f32[264,256]{1,0:T(8,128)}, u32[]{:S(2)}, u32[]{:S(2)}) collective-permute-start(f32[264,256]{1,0:T(8,128)} %pad_maximum_fusion.1), channel_id=1, source_target_pairs={{0,1},{1,2},{2,3},{3,4},{4,5},{5,6},{6,7},{7,8},{8,9},{9,10},{10,1... | collective-permute-start | bytes 811016 | tf_op jit(solution)/shard_map/ppermute | solution.py:99
  63.7 0.4 fusion.56
  64.1 0.4 fusion.58
  64.5 0.4 fusion.66
  64.9 0.6 fusion.14
  65.6 1.1 fusion.99
  66.8 0.3 fusion.110
  67.2 0.7 pad_maximum_fusion.2
  68.0 0.3 fusion.109
  68.4 0.5 copy-done
  68.9 1.0 fusion.20
  69.9 0.8 multiply_reduce_fusion.1
  71.4 0.3 fusion.25
  71.7 0.3 fusion.13
  72.3 0.3 fusion.24
  73.5 0.3 fusion.11
  74.4 1.0 fusion.21
  75.4 0.7 multiply_reduce_fusion
  76.7 0.3 fusion.23
  77.1 0.3 fusion.9
  77.6 0.3 fusion.22
  80.5 0.3 fusion.107
  80.8 0.5 fusion.4
  81.3 1.0 reshape.193
  82.3 10.7 %all-to-all-start.2 = ((bf16[64,4,1024]{2,1,0:T(4,128)(2,1)}), bf16[64,4,1024]{2,1,0:T(4,128)(2,1)S(1)}, u32[]{:S(2)}, u32[]{:S(2)}) async-start(bf16[64,4,1024]{2,1,0:T(4,128)(2,1)} %reshape.193), calls=%async_computation.2 | async-start | bytes 1048576 | tf_op jit(solution)/shard_map/all_to_all | solution.py:77
  93.8 0.3 fusion.116
  94.1 0.5 fusion.5
  94.8 15.8 %all-to-all-done.2 = bf16[64,4,1024]{2,1,0:T(4,128)(2,1)S(1)} async-done(((bf16[64,4,1024]{2,1,0:T(4,128)(2,1)}), bf16[64,4,1024]{2,1,0:T(4,128)(2,1)S(1)}, u32[]{:S(2)}, u32[]{:S(2)}) %all-to-all-start.2) | async-done | bytes 524320 | tf_op jit(solution)/shard_map/all_to_all | solution.py:77
  110.6 23.2 %all_to_all.20 = bf16[64,4,1024]{2,1,0:T(4,128)(2,1)S(1)} all-to-all(bf16[64,4,1024]{2,1,0:T(4,128)(2,1)S(1)} %reshape.194), channel_id=1, replica_groups=mesh['grp'=4,'mem'=64] {'mem'}, dimensions={0} | all-to-all | bytes 1048576 | tf_op jit(solution)/shard_map/all_to_all | solution.py:77
  133.8 0.7 pad_maximum_fusion
  134.5 1.6 %copy.9 = bf16[64,2,4,1024]{3,2,1,0:T(4,128)(2,1)} copy(bf16[64,2,4,1024]{3,2,0,1:T(4,128)(2,1)S(1)} %pad_maximum_fusion) | data formatting | bytes 2097152 | tf_op jit(solution)/shard_map/stack | solution.py:107
  (56 shorter events, 7.2 us)
Async XLA Ops:
  2.5 13.3 %copy-start.6 = (s32[2]{0:T(128)S(1)}, s32[2]{0:T(128)}, u32[]{:S(2)}) copy-start(s32[2]{0:T(128)} %param.7) | copy-start | bytes 28
  2.5 13.9 %copy-start.2 = (f32[2,1024]{1,0:T(2,128)S(1)}, f32[2,1024]{1,0:T(2,128)}, u32[]{:S(2)}) copy-start(f32[2,1024]{1,0:T(2,128)} %param.9) | copy-start | bytes 24580
  2.5 13.9 %copy-start.3 = (f32[2,1024]{1,0:T(2,128)S(1)}, f32[2,1024]{1,0:T(2,128)}, u32[]{:S(2)}) copy-start(f32[2,1024]{1,0:T(2,128)} %param.10) | copy-start | bytes 24580
  2.5 15.1 %copy-start.5 = (f32[2,1024]{1,0:T(2,128)S(1)}, f32[2,1024]{1,0:T(2,128)}, u32[]{:S(2)}) copy-start(f32[2,1024]{1,0:T(2,128)} %param.11) | copy-start | bytes 24580
  2.5 36.7 %copy-start.4 = (s32[2,1024]{1,0:T(2,128)S(1)}, s32[2,1024]{1,0:T(2,128)}, u32[]{:S(2)}) copy-start(s32[2,1024]{1,0:T(2,128)} %param.8) | copy-start | bytes 24580
  2.6 31.0 %all-to-all-start = ((bf16[64,4,1024]{2,1,0:T(4,128)(2,1)}), bf16[64,4,1024]{2,1,0:T(4,128)(2,1)S(1)}, u32[]{:S(2)}, u32[]{:S(2)}) async-start(bf16[64,4,1024]{2,1,0:T(4,128)(2,1)} %get-tuple-element.5), calls=%async_computation | async-start | bytes 1048576 | tf_op jit(solution)/shard_map/all_to_all | solution.py:77
  33.5 23.4 %all-to-all-start.1 = ((bf16[64,4,1024]{2,1,0:T(4,128)(2,1)}), bf16[64,4,1024]{2,1,0:T(4,128)(2,1)S(1)}, u32[]{:S(2)}, u32[]{:S(2)}) async-start(bf16[64,4,1024]{2,1,0:T(4,128)(2,1)} %get-tuple-element.6), calls=%async_computation.1 | async-start | bytes 1048576 | tf_op jit(solution)/shard_map/all_to_all | solution.py:77
  62.0 6.3 %collective-permute-start = (f32[264,256]{1,0:T(8,128)}, f32[264,256]{1,0:T(8,128)}, u32[]{:S(2)}, u32[]{:S(2)}) collective-permute-start(f32[264,256]{1,0:T(8,128)} %pad_maximum_fusion.1), channel_id=1, source_target_pairs={{0,1},{1,2},{2,3},{3,4},{4,5},{5,6},{6,7},{7,8},{8,9},{9,10},{10,1... | collective-permute-start | bytes 811016 | tf_op jit(solution)/shard_map/ppermute | solution.py:99
  67.9 6.5 %collective-permute-start.1 = (f32[264,256]{1,0:T(8,128)}, f32[264,256]{1,0:T(8,128)}, u32[]{:S(2)}, u32[]{:S(2)}) collective-permute-start(f32[264,256]{1,0:T(8,128)} %pad_maximum_fusion.2), channel_id=1, source_target_pairs={{1,0},{2,1},{3,2},{4,3},{5,4},{6,5},{7,6},{8,7},{9,8},{10,9},{11,1... | collective-permute-start | bytes 811016 | tf_op jit(solution)/shard_map/ppermute | solution.py:94
  67.9 1.0 copy-start
  67.9 1.0 copy-start.1
  82.3 28.4 %all-to-all-start.2 = ((bf16[64,4,1024]{2,1,0:T(4,128)(2,1)}), bf16[64,4,1024]{2,1,0:T(4,128)(2,1)S(1)}, u32[]{:S(2)}, u32[]{:S(2)}) async-start(bf16[64,4,1024]{2,1,0:T(4,128)(2,1)} %reshape.193), calls=%async_computation.2 | async-start | bytes 1048576 | tf_op jit(solution)/shard_map/all_to_all | solution.py:77

commit v2 on v1

v2 whole, which is shorter than its diff:
```python
import jax
import jax.numpy as jnp
from jax import lax
from jax.experimental import pallas as pl
from jax.experimental.pallas import tpu as pltpu
from jax.sharding import PartitionSpec as P

NSTEPS = 5
HIGHEST = lax.Precision.HIGHEST
F32 = jnp.float32
BF16 = jnp.bfloat16


def direction_weights(shift_amount):
    toward_west = jnp.exp(-((shift_amount + 0.5) ** 2))
    own_weight = jnp.exp(-((shift_amount - 0.5) ** 2))
    toward_east = jnp.exp(-((1.5 - shift_amount) ** 2))
    return (toward_west, own_weight, toward_east)


def binned(tally, slot, datum, precision, offset, values):
    slots = slot.shape[0]
    live = (jnp.arange(slots, dtype=jnp.int32) < tally).astype(F32)
    weights = jnp.stack(direction_weights(offset)) * (precision * live)[None]
    rows = jnp.concatenate([weights, weights * datum[None]], axis=0)
    chosen = (slot[:, None] == jnp.arange(values, dtype=jnp.int32)[None, :]).astype(F32)
    return jnp.dot(rows, chosen, precision=HIGHEST)


def halves(value):
    high = value.astype(BF16)
    return high, (value - high.astype(F32)).astype(BF16)


def product(left, right):
    (left_high, left_low), (right_high, right_low) = left, right
    return jnp.dot(
        jnp.concatenate([left_high, left_high, left_low], axis=1),
        jnp.concatenate([right_high, right_low, right_high], axis=0),
        preferred_element_type=F32,
    )


def against(left, right):
    return lax.dot_general(left, right, (((1,), (1,)), ((), ())), preferred_element_type=F32)


def rows_of(spread, bins, which):
    return (spread.astype(F32) * jnp.sqrt(bins[which : which + 1])).astype(BF16)


def pulls_of(spread, center, bins):
    high, low = halves(bins[3:6] - bins[0:3] * center)
    both = against(jnp.concatenate([high, low], axis=0), spread)
    return both[0:3] + both[3:6]


def outgoing_body(members_ref, bins_ref, spread_ref, center_ref, pulls_ref, west_ref, east_ref):
    peers, _, held, values = members_ref.shape
    count = peers * held
    for column, which, sent in ((0, 0, west_ref), (1, 2, east_ref)):
        wide = members_ref[:, column].astype(F32).reshape(count, values)
        center = jnp.sum(wide, axis=0, keepdims=True) * (1.0 / count)
        center_ref[column : column + 1, :] = center
        spread = (wide - center).astype(BF16)
        spread_ref[column] = spread
        bins = bins_ref[column]
        rows = rows_of(spread, bins, which)
        sent[0:count, :] = against(rows, rows).astype(BF16)
        pulls = pulls_of(spread, center, bins)
        pulls_ref[column] = pulls
        high, low = halves(pulls[which : which + 1])
        sent[count:, :] = jnp.concatenate([high, low, jnp.zeros((14, count), BF16)], axis=0)


def local_body(spread_ref, bins_ref, system_ref):
    count = spread_ref.shape[1]
    for column, other, which in ((0, 1, 0), (1, 0, 2)):
        own = rows_of(spread_ref[column], bins_ref[column], 1)
        side = rows_of(spread_ref[other], bins_ref[other], which)
        rows = jnp.concatenate([own, side], axis=1)
        system_ref[column] = against(rows, rows)


def analysis_body(
    system_ref, pulls_ref, from_west_ref, from_east_ref, spread_ref, center_ref, out_ref
):
    peers, _, held, values = out_ref.shape
    count = peers * held
    diagonal = lax.broadcasted_iota(jnp.int32, (count, count), 0) == lax.broadcasted_iota(
        jnp.int32, (count, count), 1
    )
    half_more = jnp.where(diagonal, 1.5, 0.0).astype(F32)
    eye = jnp.where(diagonal, count - 1.0, 0.0).astype(F32)
    columns = (0, 1)
    iterates, inverses, norms = [], [], []
    for column in columns:
        received = (from_west_ref, from_east_ref)[column]
        system = eye + system_ref[column] + received[0:count, :].astype(F32)
        squares = jnp.sum(jnp.sum(system * system, axis=0, keepdims=True), axis=1, keepdims=True)
        norm = jnp.sqrt(squares)
        iterate = system * (1.0 / norm)
        inverse = halves(half_more - 0.5 * iterate)
        norms.append(norm)
        inverses.append(inverse)
        iterates.append(halves(product(halves(iterate), inverse)))
    roots = [None, None]
    for step in range(1, NSTEPS):
        middles = [
            halves(half_more - 0.5 * product(inverses[column], iterates[column]))
            for column in columns
        ]
        if step < NSTEPS - 1:
            iterates = [halves(product(iterates[column], middles[column])) for column in columns]
        roots = [product(middles[column], inverses[column]) for column in columns]
        inverses = [halves(root) for root in roots]
    for column in columns:
        received = (from_west_ref, from_east_ref)[column]
        arrived = received[count:, :].astype(F32)
        pulls, others = pulls_ref[column], pulls_ref[1 - column]
        side = (0, 2)[column]
        pull = pulls[1:2] + others[side : side + 1] + arrived[0:1] + arrived[1:2]
        root = roots[column] * (1.0 / jnp.sqrt(norms[column]))
        inner = jnp.sum(root * pull, axis=1, keepdims=True)
        mean_weight = jnp.sum(root * inner, axis=0, keepdims=True)
        transform = ((count - 1.0) ** 0.5 * root + mean_weight).astype(BF16)
        grown = jnp.dot(transform, spread_ref[column], preferred_element_type=F32)
        analysis = center_ref[column : column + 1, :] + grown
        out_ref[:, column] = analysis.reshape(peers, held, values).astype(BF16)


def call(body, flops, outs, *operands):
    return pl.pallas_call(
        body,
        out_shape=outs,
        in_specs=[pl.BlockSpec(memory_space=pltpu.VMEM)] * len(operands),
        out_specs=jax.tree.map(lambda _: pl.BlockSpec(memory_space=pltpu.VMEM), outs),
        compiler_params=pltpu.CompilerParams(vmem_limit_bytes=24 << 20),
        cost_estimate=pl.CostEstimate(flops=flops, bytes_accessed=1 << 20, transcendentals=0),
    )(*operands)


def exchange(value):
    return lax.all_to_all(value, "mem", split_axis=0, concat_axis=0, tiled=True)


def per_device(background, tally, slot, datum, precision, offset):
    columns, held, values = background.shape
    peers = lax.axis_size("mem")
    count = peers * held
    members = exchange(background).reshape(peers, 2, held, values)
    bins = jnp.stack(
        [binned(tally[c], slot[c], datum[c], precision[c], offset[c], values) for c in range(2)]
    )
    shape = jax.ShapeDtypeStruct
    sent = shape((count + 16, count), BF16)
    flops = 2 * count * count * values
    spread, center, pulls, westward, eastward = call(
        outgoing_body,
        2 * flops,
        (
            shape((2, count, values), BF16),
            shape((2, values), F32),
            shape((2, 3, count), F32),
            sent,
            sent,
        ),
        members,
        bins,
    )
    total = lax.axis_size("grp") * peers
    up = [(i, (i + 1) % total) for i in range(total)]
    from_west = lax.ppermute(eastward, ("grp", "mem"), up)
    from_east = lax.ppermute(westward, ("grp", "mem"), [(b, a) for a, b in up])
    system = call(local_body, 4 * flops, shape((2, count, count), F32), spread, bins)
    analysis = call(
        analysis_body,
        2 * flops + 2 * 12 * 3 * 2 * count**3,
        shape((peers, 2, held, values), BF16),
        system,
        pulls,
        from_west,
        from_east,
        spread,
        center,
    )
    return exchange(analysis.reshape(columns, held, values))


def solution(mesh):
    both = ("grp", "mem")
    in_specs = (
        P("grp", "mem", None),
        P(both),
        P(both, None),
        P(both, None),
        P(both, None),
        P(both, None),
    )
    return jax.shard_map(
        per_device, mesh=mesh, in_specs=in_specs, out_specs=P("grp", "mem", None), check_vma=False
    )
```

time: 137 us -> 93.6 us (0.68)
  waiting for transfers between devices: 46.1 us -> 26.9 us
  blocking collectives: 23.2 us -> 38.9 us
  starting transfers between devices: 31.1 us -> 15.6 us
  matrix products: 17.5 us -> 2.93 us
  other arithmetic: 8.95 us -> 1.37 us
  Pallas kernels: 0 us -> 5.91 us
  local copies, waits for them, and re-layouts: 7.28 us -> 1.65 us
  between operations: 2.01 us -> 0.13 us
    all_to_all x3 -> x1, waiting for transfers between devices: 46.1 us -> 23.1 us  [exchange(): return lax.all_to_all(value, 'mem', split_axis=0, concat_axis=0, tiled=True)]
    all_to_all x3 -> x1, starting transfers between devices: 29.6 us -> 13.3 us  [exchange(): return lax.all_to_all(value, 'mem', split_axis=0, concat_axis=0, tiled=True)]
    all_to_all x1, blocking collectives: 23.2 us -> 38.9 us  [exchange(): return lax.all_to_all(value, 'mem', split_axis=0, concat_axis=0, tiled=True)]
    dot_general x42 -> x0, matrix products: 14.6 us -> none  [the longest x6 3.45 us: products(): lax.dot_general(rows, rows, (((1,), (1,)), ((), ())), preferred_element_t...]
    pallas_call x0 -> x3, Pallas kernels: none -> 5.91 us  [call(): pl.pallas_call(body, out_shape=outs, in_specs=[pl.BlockSpec(memory_space=...]
    ppermute x2, waiting for transfers between devices: 0.01 us -> 3.72 us  [the longest x1 2.46 us: per_device(): from_east = lax.ppermute(westward, ('grp', 'mem'), [(b, a) for a, b in up])]
    squeeze x1 -> x0, local copies, waits for them, and re-layouts: 2.52 us -> none  [per_device(): even_in = exchange(sides[:, 0])]
    add x2 -> x0, other arithmetic: 2.01 us -> none  [the longest x1 1.01 us: per_device(): odd_own + even_east + from_east]
  transfers between devices with their start and end apart: 5 -> 3, of which waited for: 3 -> 3; matrix products, arithmetic and copies ran while one was open for 12% -> 5% of each run, Pallas kernels for 0% -> 1%
where the time goes in v2:
time: 93.6 us; the launch traced here: 93.4 us
  blocking collectives  38.9 us (42%)
  waiting for transfers between devices  26.9 us (29%)
  starting transfers between devices  15.6 us (17%)
  Pallas kernels  5.91 us (6%)
  matrix products  2.93 us (3%)
  local copies, waits for them, and re-layouts  1.65 us (2%)
  other arithmetic  1.37 us (1%)
    all_to_all x1, blocking collectives, exchange(): return lax.all_to_all(value, 'mem', split_axis=0, concat_axis=0, tiled=True)  38.9 us
    all_to_all x1, waiting for transfers between devices, exchange(): return lax.all_to_all(value, 'mem', split_axis=0, concat_axis=0, tiled=True)  23.1 us
    all_to_all x1, starting transfers between devices, exchange(): return lax.all_to_all(value, 'mem', split_axis=0, concat_axis=0, tiled=True)  13.3 us
    pallas_call x3, Pallas kernels, call(): pl.pallas_call(body, out_shape=outs, in_specs=[pl.BlockSpec(memory_space=...  5.91 us
    dot_general x2, matrix products, binned(): return jnp.dot(rows, chosen, precision=HIGHEST)  2.93 us
    ppermute x1, waiting for transfers between devices, per_device(): from_east = lax.ppermute(westward, ('grp', 'mem'), [(b, a) for a, b in up])  2.46 us
    ppermute x1, starting transfers between devices, per_device(): from_west = lax.ppermute(eastward, ('grp', 'mem'), up)  2.31 us
  transfers between devices with their start and end apart: 3, of which 3 were waited for; matrix products, arithmetic and copies ran while one was open for 5% of the time, Pallas kernels for 1%

profile of v2, /device:TPU:1, one launch (start us, length us, event | category | flops | bytes accessed | tf_op | source)
XLA Modules:
  0.0 93.4 jit_solution(17021817206829612421)
XLA Ops:
  0.0 0.0 copy-start.4
  0.0 0.0 copy-start
  0.0 0.0 copy-start.1
  0.0 0.0 copy-start.2
  0.0 0.0 copy-start.3
  0.0 13.3 %all-to-all-start = ((bf16[128,4,1024]{2,1,0:T(4,128)(2,1)}), bf16[128,4,1024]{2,1,0:T(4,128)(2,1)S(1)}, u32[]{:S(2)}, u32[]{:S(2)}) async-start(bf16[128,4,1024]{2,1,0:T(4,128)(2,1)} %param.6), calls=%async_computation | async-start | bytes 2097152 | tf_op jit(solution)/shard_map/all_to_all | solution.py:144
  13.3 0.0 copy-done.4
  13.3 0.6 fusion.16
  14.0 0.0 copy-done
  14.0 0.0 copy-done.1
  14.0 0.0 copy-done.2
  14.0 1.3 %compare_select_fusion.1 = (f32[1,1024]{1,0:T(1,128)S(1)}, f32[1,1024]{1,0:T(1,128)S(1)}) fusion(f32[2,1024]{1,0:T(2,128)S(1)} %copy-done.2, s32[]{:T(128)} %bitcast.1, s32[]{:T(128)} %bitcast.6), kind=kLoop, calls=%fused_computation.18 | loop fusion | flops 4096 | bytes 16392 | tf_op jit(solution)/shard_map/mul | solution.py:24
  15.3 0.0 copy-done.3
  15.4 1.5 %fusion.5 = f32[1,6,1024]{2,1,0:T(8,128)S(1)} fusion(s32[1024]{0:T(1024)S(1)} %bitcast.21, f32[3,1024]{1,0:T(4,128)S(1)} %get-tuple-element.16, f32[3,1024]{1,0:T(4,128)S(1)} %get-tuple-element.15), kind=kOutput, calls=%fused_computation.7 | convolution fusion | flops 76552192 | bytes 53248 | tf_op jit(solution)/shard_map/dot_general | solution.py:27
  16.9 1.5 %fusion.4 = f32[1,6,1024]{2,1,0:T(8,128)S(1)} fusion(s32[1024]{0:T(1024)S(1)} %bitcast.20, f32[3,1024]{1,0:T(4,128)S(1)} %get-tuple-element.33, f32[3,1024]{1,0:T(4,128)S(1)} %get-tuple-element.34), kind=kOutput, calls=%fused_computation.6 | convolution fusion | flops 76552192 | bytes 53248 | tf_op jit(solution)/shard_map/dot_general | solution.py:27
  18.4 23.1 %all-to-all-done = bf16[128,4,1024]{2,1,0:T(4,128)(2,1)S(1)} async-done(((bf16[128,4,1024]{2,1,0:T(4,128)(2,1)}), bf16[128,4,1024]{2,1,0:T(4,128)(2,1)S(1)}, u32[]{:S(2)}, u32[]{:S(2)}) %all-to-all-start) | async-done | bytes 1048608 | tf_op jit(solution)/shard_map/all_to_all | solution.py:144
  41.5 0.9 shard_map.64
  42.4 2.3 %collective-permute-start = (bf16[272,256]{1,0:T(8,128)(2,1)S(1)}, bf16[272,256]{1,0:T(8,128)(2,1)S(1)}, u32[]{:S(2)}, u32[]{:S(2)}) collective-permute-start(bf16[272,256]{1,0:T(8,128)(2,1)S(1)} %get-tuple-element.12), channel_id=1, source_target_pairs={{0,1},{1,2},{2,3},{3,4},{4,5},{5,6},{6,7},{7,8},{8,9},{9,10},{10,1... | collective-permute-start | bytes 417800 | tf_op jit(solution)/shard_map/ppermute | solution.py:173
  44.7 0.0 collective-permute-start.1
  44.7 0.7 shard_map.65.system_ref
  45.5 1.3 %collective-permute-done.from_west_ref = bf16[272,256]{1,0:T(8,128)(2,1)S(1)} collective-permute-done((bf16[272,256]{1,0:T(8,128)(2,1)S(1)}, bf16[272,256]{1,0:T(8,128)(2,1)S(1)}, u32[]{:S(2)}, u32[]{:S(2)}) %collective-permute-start) | collective-permute-done | bytes 139296 | tf_op jit(solution)/shard_map/ppermute | solution.py:173
  46.8 2.5 %collective-permute-done.1.from_east_ref = bf16[272,256]{1,0:T(8,128)(2,1)S(1)} collective-permute-done((bf16[272,256]{1,0:T(8,128)(2,1)S(1)}, bf16[272,256]{1,0:T(8,128)(2,1)S(1)}, u32[]{:S(2)}, u32[]{:S(2)}) %collective-permute-start.1) | collective-permute-done | bytes 139296 | tf_op jit(solution)/shard_map/ppermute | solution.py:174
  49.2 4.2 %shard_map.66 = bf16[64,2,4,1024]{3,2,1,0:T(4,128)(2,1)S(1)} custom-call(f32[2,256,256]{2,1,0:T(8,128)S(1)} %shard_map.65.system_ref, f32[2,3,256]{2,1,0:T(4,128)S(1)} %get-tuple-element.11.pulls_ref, bf16[272,256]{1,0:T(8,128)(2,1)S(1)} %collective-permute-done.from_west_ref, bf16[272,256]{1,0:T(8,128)(2,1)S(1)} %collective-permute-done.1.from_east_ref, ...), custom_call_target="tpu_custom_call" | custom-call | flops 2684354560 | bytes 1048576 | tf_op jit(solution)/shard_map/pallas_call | solution.py:133
  53.5 38.9 %all_to_all.10 = bf16[128,4,1024]{2,1,0:T(4,128)(2,1)S(1)} all-to-all(bf16[128,4,1024]{2,1,0:T(4,128)(2,1)S(1)} %bitcast.15), channel_id=1, replica_groups=mesh['grp'=4,'mem'=64] {'mem'}, dimensions={0} | all-to-all | bytes 2097152 | tf_op jit(solution)/shard_map/all_to_all | solution.py:144
  92.4 1.0 %copy.8 = bf16[128,4,1024]{2,1,0:T(4,128)(2,1)} copy(bf16[128,4,1024]{2,1,0:T(4,128)(2,1)S(1)} %all_to_all.10) | data formatting | bytes 2097152
  (5 shorter events, 0.1 us)
Async XLA Ops:
  0.0 13.3 %copy-start.4 = (s32[2]{0:T(128)S(1)}, s32[2]{0:T(128)}, u32[]{:S(2)}) copy-start(s32[2]{0:T(128)} %param.7) | copy-start | bytes 28
  0.0 14.0 %copy-start = (s32[2,1024]{1,0:T(2,128)S(1)}, s32[2,1024]{1,0:T(2,128)}, u32[]{:S(2)}) copy-start(s32[2,1024]{1,0:T(2,128)} %param.8) | copy-start | bytes 24580
  0.0 14.0 %copy-start.1 = (f32[2,1024]{1,0:T(2,128)S(1)}, f32[2,1024]{1,0:T(2,128)}, u32[]{:S(2)}) copy-start(f32[2,1024]{1,0:T(2,128)} %param.9) | copy-start | bytes 24580
  0.0 14.0 %copy-start.2 = (f32[2,1024]{1,0:T(2,128)S(1)}, f32[2,1024]{1,0:T(2,128)}, u32[]{:S(2)}) copy-start(f32[2,1024]{1,0:T(2,128)} %param.10) | copy-start | bytes 24580
  0.0 15.3 %copy-start.3 = (f32[2,1024]{1,0:T(2,128)S(1)}, f32[2,1024]{1,0:T(2,128)}, u32[]{:S(2)}) copy-start(f32[2,1024]{1,0:T(2,128)} %param.11) | copy-start | bytes 24580
  0.0 41.5 %all-to-all-start = ((bf16[128,4,1024]{2,1,0:T(4,128)(2,1)}), bf16[128,4,1024]{2,1,0:T(4,128)(2,1)S(1)}, u32[]{:S(2)}, u32[]{:S(2)}) async-start(bf16[128,4,1024]{2,1,0:T(4,128)(2,1)} %param.6), calls=%async_computation | async-start | bytes 2097152 | tf_op jit(solution)/shard_map/all_to_all | solution.py:144
  42.4 4.3 %collective-permute-start = (bf16[272,256]{1,0:T(8,128)(2,1)S(1)}, bf16[272,256]{1,0:T(8,128)(2,1)S(1)}, u32[]{:S(2)}, u32[]{:S(2)}) collective-permute-start(bf16[272,256]{1,0:T(8,128)(2,1)S(1)} %get-tuple-element.12), channel_id=1, source_target_pairs={{0,1},{1,2},{2,3},{3,4},{4,5},{5,6},{6,7},{7,8},{8,9},{9,10},{10,1... | collective-permute-start | bytes 417800 | tf_op jit(solution)/shard_map/ppermute | solution.py:173
  44.7 4.5 %collective-permute-start.1 = (bf16[272,256]{1,0:T(8,128)(2,1)S(1)}, bf16[272,256]{1,0:T(8,128)(2,1)S(1)}, u32[]{:S(2)}, u32[]{:S(2)}) collective-permute-start(bf16[272,256]{1,0:T(8,128)(2,1)S(1)} %get-tuple-element.13), channel_id=1, source_target_pairs={{1,0},{2,1},{3,2},{4,3},{5,4},{6,5},{7,6},{8,7},{9,8},{10,9},{11,1... | collective-permute-start | bytes 417800 | tf_op jit(solution)/shard_map/ppermute | solution.py:174

commit v3 on v2

--- a/solution.py
+++ b/solution.py
@@ -1,11 +1,13 @@
 import jax
 import jax.numpy as jnp
+import numpy as np
 from jax import lax
 from jax.experimental import pallas as pl
 from jax.experimental.pallas import tpu as pltpu
 from jax.sharding import PartitionSpec as P
 
-NSTEPS = 5
+
+BOTH = ("grp", "mem")
 HIGHEST = lax.Precision.HIGHEST
 F32 = jnp.float32
 BF16 = jnp.bfloat16
@@ -18,13 +20,23 @@
     return (toward_west, own_weight, toward_east)
 
 
-def binned(tally, slot, datum, precision, offset, values):
-    slots = slot.shape[0]
-    live = (jnp.arange(slots, dtype=jnp.int32) < tally).astype(F32)
-    weights = jnp.stack(direction_weights(offset)) * (precision * live)[None]
+def binned(observations, values):
+    slot, datum, precision, offset = observations
+    weights = jnp.stack(direction_weights(offset)) * precision[None]
     rows = jnp.concatenate([weights, weights * datum[None]], axis=0)
-    chosen = (slot[:, None] == jnp.arange(values, dtype=jnp.int32)[None, :]).astype(F32)
+    picks = slot.astype(jnp.int32)
+    chosen = (picks[:, None] == jnp.arange(values, dtype=jnp.int32)[None, :]).astype(F32)
     return jnp.dot(rows, chosen, precision=HIGHEST)
+
+
+def walk():
+    chips = [row * 4 + (place, 3 - place)[row % 2] for row in range(8) for place in range(4)]
+    return [0] + [2 * chip + core for chip in chips[1:] for core in (0, 1)] + [1]
+
+
+def two_step_factors():
+    root = max(np.roots([1.0, -6.0, 9.0, -12.0]), key=np.real).real
+    return (-(3.0 + root) / 4, 3.0 * root / 4), ((root - 6.0) / 4, 3.0 / root)
 
 
 def halves(value):
@@ -74,7 +86,6 @@
 
 
 def local_body(spread_ref, bins_ref, system_ref):
-    count = spread_ref.shape[1]
     for column, other, which in ((0, 1, 0), (1, 0, 2)):
         own = rows_of(spread_ref[column], bins_ref[column], 1)
         side = rows_of(spread_ref[other], bins_ref[other], which)
@@ -90,30 +101,44 @@
     diagonal = lax.broadcasted_iota(jnp.int32, (count, count), 0) == lax.broadcasted_iota(
         jnp.int32, (count, count), 1
     )
-    half_more = jnp.where(diagonal, 1.5, 0.0).astype(F32)
-    eye = jnp.where(diagonal, count - 1.0, 0.0).astype(F32)
+
+    def scaled_eye(value):
+        return jnp.where(diagonal, value, 0.0).astype(F32)
+
     columns = (0, 1)
-    iterates, inverses, norms = [], [], []
+    quadratics = [(linear, scaled_eye(constant)) for linear, constant in two_step_factors()]
+
+    def two_steps(ratios):
+        split = [halves(ratio) for ratio in ratios]
+        squares = [0.25 * product(x, x) for x in split]
+        factors = [
+            [halves(square + linear * ratio + constant) for linear, constant in quadratics]
+            for square, ratio in zip(squares, ratios)
+        ]
+        return split, [halves(product(*pair)) for pair in factors]
+
+    def advanced(split, gains):
+        twice = [halves(product(gain, gain)) for gain in gains]
+        return [product(x, gain) for x, gain in zip(split, twice)]
+
+    norms, ratios = [], []
     for column in columns:
         received = (from_west_ref, from_east_ref)[column]
-        system = eye + system_ref[column] + received[0:count, :].astype(F32)
+        system = scaled_eye(count - 1.0) + system_ref[column] + received[0:count, :].astype(F32)
         squares = jnp.sum(jnp.sum(system * system, axis=0, keepdims=True), axis=1, keepdims=True)
         norm = jnp.sqrt(squares)
-        iterate = system * (1.0 / norm)
-        inverse = halves(half_more - 0.5 * iterate)
         norms.append(norm)
-        inverses.append(inverse)
-        iterates.append(halves(product(halves(iterate), inverse)))
-    roots = [None, None]
-    for step in range(1, NSTEPS):
-        middles = [
-            halves(half_more - 0.5 * product(inverses[column], iterates[column]))
-            for column in columns
-        ]
-        if step < NSTEPS - 1:
-            iterates = [halves(product(iterates[column], middles[column])) for column in columns]
-        roots = [product(middles[column], inverses[column]) for column in columns]
-        inverses = [halves(root) for root in roots]
+        ratios.append(system * (1.0 / norm))
+    split, first = two_steps(ratios)
+    ratios = advanced(split, first)
+    split, second = two_steps(ratios)
+    inverses = [halves(product(*pair)) for pair in zip(first, second)]
+    ratios = advanced(split, second)
+    half_more = scaled_eye(1.5)
+    roots = [
+        product(halves(half_more - 0.5 * ratio), inverse)
+        for ratio, inverse in zip(ratios, inverses)
+    ]
     for column in columns:
         received = (from_west_ref, from_east_ref)[column]
         arrived = received[count:, :].astype(F32)
@@ -141,17 +166,25 @@
 
 
 def exchange(value):
-    return lax.all_to_all(value, "mem", split_axis=0, concat_axis=0, tiled=True)
-
-
-def per_device(background, tally, slot, datum, precision, offset):
+    return lax.all_to_all(
+        value, "mem", split_axis=0, concat_axis=0, tiled=True, axis_index_groups=[walk()]
+    )
+
+
+def analyse(background, tally, slot, datum, precision, offset):
     columns, held, values = background.shape
-    peers = lax.axis_size("mem")
+    peers, groups = lax.axis_size("mem"), lax.axis_size("grp")
     count = peers * held
+    order = walk()
     members = exchange(background).reshape(peers, 2, held, values)
-    bins = jnp.stack(
-        [binned(tally[c], slot[c], datum[c], precision[c], offset[c], values) for c in range(2)]
-    )
+    live = jnp.arange(values, dtype=jnp.int32)[None, :] < tally[:, None]
+    observations = jnp.stack(
+        [slot.astype(F32), datum, precision * live.astype(F32), offset], axis=0
+    )
+    observations = lax.ppermute(
+        observations.reshape(8, values), "mem", [(p, order[p]) for p in range(peers)]
+    ).reshape(4, 2, values)
+    bins = jnp.stack([binned(observations[:, c], values) for c in range(2)])
     shape = jax.ShapeDtypeStruct
     sent = shape((count + 16, count), BF16)
     flops = 2 * count * count * values
@@ -168,14 +201,14 @@
         members,
         bins,
     )
-    total = lax.axis_size("grp") * peers
-    up = [(i, (i + 1) % total) for i in range(total)]
-    from_west = lax.ppermute(eastward, ("grp", "mem"), up)
-    from_east = lax.ppermute(westward, ("grp", "mem"), [(b, a) for a, b in up])
+    ring = [group * peers + place for group in range(groups) for place in order]
+    up = list(zip(ring, ring[1:] + ring[:1]))
+    from_west = lax.ppermute(eastward, BOTH, up)
+    from_east = lax.ppermute(westward, BOTH, [(b, a) for a, b in up])
     system = call(local_body, 4 * flops, shape((2, count, count), F32), spread, bins)
     analysis = call(
         analysis_body,
-        2 * flops + 2 * 12 * 3 * 2 * count**3,
+        2 * flops + 2 * 10 * 3 * 2 * count**3,
         shape((peers, 2, held, values), BF16),
         system,
         pulls,
@@ -188,15 +221,14 @@
 
 
 def solution(mesh):
-    both = ("grp", "mem")
     in_specs = (
         P("grp", "mem", None),
-        P(both),
-        P(both, None),
-        P(both, None),
-        P(both, None),
-        P(both, None),
+        P(BOTH),
+        P(BOTH, None),
+        P(BOTH, None),
+        P(BOTH, None),
+        P(BOTH, None),
     )
     return jax.shard_map(
-        per_device, mesh=mesh, in_specs=in_specs, out_specs=P("grp", "mem", None), check_vma=False
-    )
+        analyse, mesh=mesh, in_specs=in_specs, out_specs=P("grp", "mem", None), check_vma=False
+    )

time: 93.6 us -> 91.2 us (0.974)
  starting transfers between devices: 15.6 us -> 19.6 us
  blocking collectives: 38.9 us -> 35.5 us
  waiting for transfers between devices: 26.9 us -> 25.7 us
  other arithmetic: 1.37 us -> 0.2 us
    all_to_all x1, waiting for transfers between devices: 23.1 us -> 0.01 us  [exchange(): lax.all_to_all(value, 'mem', split_axis=0, concat_axis=0, tiled=True, axi...]
    ppermute x2 -> x3, waiting for transfers between devices: 3.72 us -> 25.7 us  [the longest x1 23.9 us: analyse(): lax.ppermute(observations.reshape(8, values), 'mem', [(p, order[p]) for p...]
    ppermute x2 -> x3, starting transfers between devices: 2.31 us -> 5.98 us  [the longest x1 3.23 us: analyse(): lax.ppermute(observations.reshape(8, values), 'mem', [(p, order[p]) for p...]
    all_to_all x1, blocking collectives: 38.9 us -> 35.5 us  [exchange(): lax.all_to_all(value, 'mem', split_axis=0, concat_axis=0, tiled=True, axi...]
    mul x2 -> x1, other arithmetic: 1.32 us -> 0.04 us  [binned(): weights = jnp.stack(direction_weights(offset)) * precision[None]]
  transfers between devices with their start and end apart: 3 -> 4, of which waited for: 3 -> 2; matrix products, arithmetic and copies ran while one was open for 5% -> 3% of each run, Pallas kernels for 1% -> 1%
where the time goes in v3:
time: 91.2 us; the launch traced here: 90.9 us
  blocking collectives  35.5 us (39%)
  waiting for transfers between devices  25.7 us (28%)
  starting transfers between devices  19.6 us (21%)
  Pallas kernels  5.85 us (6%)
  matrix products  2.93 us (3%)
  local copies, waits for them, and re-layouts  1.04 us (1%)
    all_to_all x1, blocking collectives, exchange(): lax.all_to_all(value, 'mem', split_axis=0, concat_axis=0, tiled=True, axi...  35.5 us
    ppermute x1, waiting for transfers between devices, analyse(): lax.ppermute(observations.reshape(8, values), 'mem', [(p, order[p]) for p...  23.9 us
    all_to_all x1, starting transfers between devices, exchange(): lax.all_to_all(value, 'mem', split_axis=0, concat_axis=0, tiled=True, axi...  13.6 us
    pallas_call x3, Pallas kernels, call(): pl.pallas_call(body, out_shape=outs, in_specs=[pl.BlockSpec(memory_space=...  5.85 us
    ppermute x1, starting transfers between devices, analyse(): lax.ppermute(observations.reshape(8, values), 'mem', [(p, order[p]) for p...  3.23 us
    dot_general x2, matrix products, binned(): return jnp.dot(rows, chosen, precision=HIGHEST)  2.93 us
    ppermute x1, starting transfers between devices, analyse(): from_east = lax.ppermute(westward, BOTH, [(b, a) for a, b in up])  2.66 us
  transfers between devices with their start and end apart: 4, of which 2 were waited for; matrix products, arithmetic and copies ran while one was open for 3% of the time, Pallas kernels for 1%

profile of v3, /device:TPU:1, one launch (start us, length us, event | category | flops | bytes accessed | tf_op | source)
XLA Modules:
  0.0 90.9 jit_solution(13696127054348113326)
XLA Ops:
  0.0 0.0 copy-start
  0.0 0.0 copy-start.1
  0.0 0.0 copy-start.4
  0.0 0.0 copy-start.2
  0.0 0.0 copy-start.3
  0.0 13.6 %all-to-all-start = ((bf16[128,4,1024]{2,1,0:T(4,128)(2,1)}), bf16[128,4,1024]{2,1,0:T(4,128)(2,1)S(1)}, u32[]{:S(2)}, u32[]{:S(2)}) async-start(bf16[128,4,1024]{2,1,0:T(4,128)(2,1)} %param.6), calls=%async_computation | async-start | bytes 2097152 | tf_op jit(solution)/shard_map/all_to_all | solution.py:169
  13.6 0.0 copy-done
  13.7 0.0 copy-done.1
  13.7 0.0 copy-done.4
  13.7 0.1 fusion.12
  13.8 0.0 copy-done.2
  13.8 0.0 copy-done.3
  13.8 3.2 %collective-permute-start = (f32[8,1024]{1,0:T(8,128)S(1)}, f32[8,1024]{1,0:T(8,128)S(1)}, u32[]{:S(2)}, u32[]{:S(2)}) collective-permute-start(f32[8,1024]{1,0:T(8,128)S(1)} %reshape.186), channel_id=1, source_target_pairs={{0,0},{1,2},{2,3},{3,4},{4,5},{5,6},{6,7},{7,14},{8,15},{9,12},{10... | collective-permute-start | bytes 98312 | tf_op jit(solution)/shard_map/ppermute | solution.py:184
  17.0 23.9 %collective-permute-done = f32[8,1024]{1,0:T(8,128)S(1)} collective-permute-done((f32[8,1024]{1,0:T(8,128)S(1)}, f32[8,1024]{1,0:T(8,128)S(1)}, u32[]{:S(2)}, u32[]{:S(2)}) %collective-permute-start) | collective-permute-done | bytes 32800 | tf_op jit(solution)/shard_map/ppermute | solution.py:184
  41.0 0.1 exponential_bitcast_fusion.5
  41.1 1.5 %fusion.5 = f32[1,6,1024]{2,1,0:T(8,128)S(1)} fusion(s32[1024]{0:T(1024)S(1)} %bitcast.39, f32[3,1024]{1,0:T(4,128)S(1)} %get-tuple-element.28, f32[3,1024]{1,0:T(4,128)S(1)} %get-tuple-element.27), kind=kOutput, calls=%fused_computation.7 | convolution fusion | flops 76552192 | bytes 53248 | tf_op jit(solution)/shard_map/dot_general | solution.py:29
  42.5 1.5 %fusion.4 = f32[1,6,1024]{2,1,0:T(8,128)S(1)} fusion(s32[1024]{0:T(1024)S(1)} %bitcast.38, f32[3,1024]{1,0:T(4,128)S(1)} %get-tuple-element.31, f32[3,1024]{1,0:T(4,128)S(1)} %get-tuple-element.32), kind=kOutput, calls=%fused_computation.6 | convolution fusion | flops 76552192 | bytes 53248 | tf_op jit(solution)/shard_map/dot_general | solution.py:29
  44.0 0.0 all-to-all-done
  44.0 0.9 %shard_map.64 = (bf16[2,256,1024]{2,1,0:T(8,128)(2,1)S(1)}, f32[2,1024]{1,0:T(2,128)S(1)}, f32[2,3,256]{2,1,0:T(4,128)S(1)}, bf16[272,256]{1,0:T(8,128)(2,1)S(1)}, bf16[272,256]{1,0:T(8,128)(2,1)S(1)}) custom-call(bf16[64,2,4,1024]{3,2,1,0:T(4,128)(2,1)S(1)} %bitcast.30, f32[2,6,1024]{2,1,0:T(8,128)S(1)} %pad_maximum_fusion.bins_ref), custom_call_target="tpu_custom_call" | custom-call | flops 268435456 | bytes 1048576 | tf_op jit(solution)/shard_map/pallas_call | solution.py:158
  45.0 0.1 collective-permute-start.1
  45.1 2.7 %collective-permute-start.2 = (bf16[272,256]{1,0:T(8,128)(2,1)S(1)}, bf16[272,256]{1,0:T(8,128)(2,1)S(1)}, u32[]{:S(2)}, u32[]{:S(2)}) collective-permute-start(bf16[272,256]{1,0:T(8,128)(2,1)S(1)} %get-tuple-element.13), channel_id=1, source_target_pairs={{2,0},{3,2},{4,3},{5,4},{6,5},{7,6},{14,7},{15,14},{12,15},{13,12}... | collective-permute-start | bytes 417800 | tf_op jit(solution)/shard_map/ppermute | solution.py:207
  47.7 0.7 shard_map.65.system_ref
  48.5 1.8 %collective-permute-done.1.from_west_ref = bf16[272,256]{1,0:T(8,128)(2,1)S(1)} collective-permute-done((bf16[272,256]{1,0:T(8,128)(2,1)S(1)}, bf16[272,256]{1,0:T(8,128)(2,1)S(1)}, u32[]{:S(2)}, u32[]{:S(2)}) %collective-permute-start.1) | collective-permute-done | bytes 139296 | tf_op jit(solution)/shard_map/ppermute | solution.py:206
  50.3 0.0 collective-permute-done.2.from_east_ref
  50.3 4.2 %shard_map.66 = bf16[64,2,4,1024]{3,2,1,0:T(4,128)(2,1)S(1)} custom-call(f32[2,256,256]{2,1,0:T(8,128)S(1)} %shard_map.65.system_ref, f32[2,3,256]{2,1,0:T(4,128)S(1)} %get-tuple-element.11.pulls_ref, bf16[272,256]{1,0:T(8,128)(2,1)S(1)} %collective-permute-done.1.from_west_ref, bf16[272,256]{1,0:T(8,128)(2,1)S(1)} %collective-permute-done.2.from_east_ref, ...), custom_call_target="tpu_custom_call" | custom-call | flops 2281701376 | bytes 1048576 | tf_op jit(solution)/shard_map/pallas_call | solution.py:158
  54.5 35.5 %all_to_all.10 = bf16[128,4,1024]{2,1,0:T(4,128)(2,1)S(1)} all-to-all(bf16[128,4,1024]{2,1,0:T(4,128)(2,1)S(1)} %bitcast.31), channel_id=1, replica_groups={{0,2,3,4,5,6,7,14,15,12,13,10,11,8,9,16,17,18,19,20,21,22,23,30,31,28,2..., dimensions={0} | all-to-all | bytes 2097152 | tf_op jit(solution)/shard_map/all_to_all | solution.py:169
  89.9 1.0 %copy.8 = bf16[128,4,1024]{2,1,0:T(4,128)(2,1)} copy(bf16[128,4,1024]{2,1,0:T(4,128)(2,1)S(1)} %all_to_all.10) | data formatting | bytes 2097152
  (6 shorter events, 0.1 us)
Async XLA Ops:
  0.0 13.6 %copy-start = (s32[2,1024]{1,0:T(2,128)S(1)}, s32[2,1024]{1,0:T(2,128)}, u32[]{:S(2)}) copy-start(s32[2,1024]{1,0:T(2,128)} %param.8) | copy-start | bytes 24580
  0.0 13.7 %copy-start.1 = (f32[2,1024]{1,0:T(2,128)S(1)}, f32[2,1024]{1,0:T(2,128)}, u32[]{:S(2)}) copy-start(f32[2,1024]{1,0:T(2,128)} %param.10) | copy-start | bytes 24580
  0.0 13.7 %copy-start.4 = (s32[2]{0:T(128)S(1)}, s32[2]{0:T(128)}, u32[]{:S(2)}) copy-start(s32[2]{0:T(128)} %param.7) | copy-start | bytes 28
  0.0 13.7 %copy-start.2 = (f32[2,1024]{1,0:T(2,128)S(1)}, f32[2,1024]{1,0:T(2,128)}, u32[]{:S(2)}) copy-start(f32[2,1024]{1,0:T(2,128)} %param.11) | copy-start | bytes 24580
  0.0 13.7 %copy-start.3 = (f32[2,1024]{1,0:T(2,128)S(1)}, f32[2,1024]{1,0:T(2,128)}, u32[]{:S(2)}) copy-start(f32[2,1024]{1,0:T(2,128)} %param.9) | copy-start | bytes 24580
  0.0 44.0 %all-to-all-start = ((bf16[128,4,1024]{2,1,0:T(4,128)(2,1)}), bf16[128,4,1024]{2,1,0:T(4,128)(2,1)S(1)}, u32[]{:S(2)}, u32[]{:S(2)}) async-start(bf16[128,4,1024]{2,1,0:T(4,128)(2,1)} %param.6), calls=%async_computation | async-start | bytes 2097152 | tf_op jit(solution)/shard_map/all_to_all | solution.py:169
  13.8 27.1 %collective-permute-start = (f32[8,1024]{1,0:T(8,128)S(1)}, f32[8,1024]{1,0:T(8,128)S(1)}, u32[]{:S(2)}, u32[]{:S(2)}) collective-permute-start(f32[8,1024]{1,0:T(8,128)S(1)} %reshape.186), channel_id=1, source_target_pairs={{0,0},{1,2},{2,3},{3,4},{4,5},{5,6},{6,7},{7,14},{8,15},{9,12},{10... | collective-permute-start | bytes 98312 | tf_op jit(solution)/shard_map/ppermute | solution.py:184
  45.0 5.3 %collective-permute-start.1 = (bf16[272,256]{1,0:T(8,128)(2,1)S(1)}, bf16[272,256]{1,0:T(8,128)(2,1)S(1)}, u32[]{:S(2)}, u32[]{:S(2)}) collective-permute-start(bf16[272,256]{1,0:T(8,128)(2,1)S(1)} %get-tuple-element.12), channel_id=1, source_target_pairs={{0,2},{2,3},{3,4},{4,5},{5,6},{6,7},{7,14},{14,15},{15,12},{12,13}... | collective-permute-start | bytes 417800 | tf_op jit(solution)/shard_map/ppermute | solution.py:206
  45.1 5.2 %collective-permute-start.2 = (bf16[272,256]{1,0:T(8,128)(2,1)S(1)}, bf16[272,256]{1,0:T(8,128)(2,1)S(1)}, u32[]{:S(2)}, u32[]{:S(2)}) collective-permute-start(bf16[272,256]{1,0:T(8,128)(2,1)S(1)} %get-tuple-element.13), channel_id=1, source_target_pairs={{2,0},{3,2},{4,3},{5,4},{6,5},{7,6},{14,7},{15,14},{12,15},{13,12}... | collective-permute-start | bytes 417800 | tf_op jit(solution)/shard_map/ppermute | solution.py:207

commit v4 on v3

v4 whole, which is shorter than its diff:
```python
import jax
import jax.numpy as jnp
import numpy as np
from jax import lax
from jax.experimental import pallas as pl
from jax.experimental.pallas import tpu as pltpu
from jax.sharding import PartitionSpec as P


BOTH = ("grp", "mem")
HIGHEST = lax.Precision.HIGHEST
F32 = jnp.float32
BF16 = jnp.bfloat16


def direction_weights(shift_amount):
    toward_west = jnp.exp(-((shift_amount + 0.5) ** 2))
    own_weight = jnp.exp(-((shift_amount - 0.5) ** 2))
    toward_east = jnp.exp(-((1.5 - shift_amount) ** 2))
    return (toward_west, own_weight, toward_east)


def binned(observations, values):
    slot, datum, precision, offset = observations
    weights = jnp.stack(direction_weights(offset)) * precision[None]
    rows = jnp.concatenate([weights, weights * datum[None]], axis=0)
    picks = slot.astype(jnp.int32)
    chosen = (picks[:, None] == jnp.arange(values, dtype=jnp.int32)[None, :]).astype(F32)
    return jnp.dot(rows, chosen, precision=HIGHEST)


def walk():
    chips = [row * 4 + (place, 3 - place)[row % 2] for row in range(8) for place in range(4)]
    return [2 * chip + core for chip in chips for core in (0, 1)]


def two_step_factors():
    root = max(np.roots([1.0, -6.0, 9.0, -12.0]), key=np.real).real
    return (-(3.0 + root) / 4, 3.0 * root / 4), ((root - 6.0) / 4, 3.0 / root)


def halves(value):
    high = value.astype(BF16)
    return high, (value - high.astype(F32)).astype(BF16)


def product(left, right):
    (left_high, left_low), (right_high, right_low) = left, right
    return jnp.dot(
        jnp.concatenate([left_high, left_high, left_low], axis=1),
        jnp.concatenate([right_high, right_low, right_high], axis=0),
        preferred_element_type=F32,
    )


def against(left, right):
    return lax.dot_general(left, right, (((1,), (1,)), ((), ())), preferred_element_type=F32)


def rows_of(spread, bins, which):
    return (spread.astype(F32) * jnp.sqrt(bins[which : which + 1])).astype(BF16)


def pulls_of(spread, center, bins):
    high, low = halves(bins[3:6] - bins[0:3] * center)
    both = against(jnp.concatenate([high, low], axis=0), spread)
    return both[0:3] + both[3:6]


def outgoing_body(
    parity_ref, members_ref, bins_ref, spread_ref, center_ref, pulls_ref, chip_ref, next_ref
):
    peers, _, held, values = members_ref.shape
    count = peers * held
    for column in (0, 1):
        wide = members_ref[:, column].astype(F32).reshape(count, values)
        center = jnp.sum(wide, axis=0, keepdims=True) * (1.0 / count)
        center_ref[column] = center
        spread = (wide - center).astype(BF16)
        spread_ref[column] = spread
        pulls_ref[column] = pulls_of(spread, center, bins_ref[column])
    parity = parity_ref[0]
    for column, sent in ((parity, next_ref), (1 - parity, chip_ref)):
        even = column == 0
        bins, pulls = bins_ref[column], pulls_ref[column]
        scale = jnp.sqrt(jnp.where(even, bins[0:1], bins[2:3]))
        rows = (spread_ref[column].astype(F32) * scale).astype(BF16)
        sent[0:count, :] = against(rows, rows).astype(BF16)
        high, low = halves(jnp.where(even, pulls[0:1], pulls[2:3]))
        sent[count:, :] = jnp.concatenate([high, low, jnp.zeros((14, count), BF16)], axis=0)


def local_body(spread_ref, bins_ref, system_ref):
    for column, other, which in ((0, 1, 0), (1, 0, 2)):
        own = rows_of(spread_ref[column], bins_ref[column], 1)
        side = rows_of(spread_ref[other], bins_ref[other], which)
        rows = jnp.concatenate([own, side], axis=1)
        system_ref[column] = against(rows, rows)


def analysis_of(column, system_ref, pulls_ref, received_ref, spread_ref, center_ref, out_ref):
    peers, _, held, values = out_ref.shape
    count = peers * held
    diagonal = lax.broadcasted_iota(jnp.int32, (count, count), 0) == lax.broadcasted_iota(
        jnp.int32, (count, count), 1
    )

    def scaled_eye(value):
        return jnp.where(diagonal, value, 0.0).astype(F32)

    def two_steps(ratio):
        split = halves(ratio)
        square = 0.25 * product(split, split)
        factors = [
            halves(square + linear * ratio + scaled_eye(constant))
            for linear, constant in two_step_factors()
        ]
        return split, halves(product(*factors))

    def advanced(split, gain):
        return product(split, halves(product(gain, gain)))

    system = scaled_eye(count - 1.0) + system_ref[column] + received_ref[0:count, :].astype(F32)
    squares = jnp.sum(jnp.sum(system * system, axis=0, keepdims=True), axis=1, keepdims=True)
    norm = jnp.sqrt(squares)
    split, first = two_steps(system * (1.0 / norm))
    split, second = two_steps(advanced(split, first))
    inverse = halves(product(first, second))
    last = halves(scaled_eye(1.5) - 0.5 * advanced(split, second))
    root = product(last, inverse) * (1.0 / jnp.sqrt(norm))
    arrived = received_ref[count:, :].astype(F32)
    pulls, others = pulls_ref[column], pulls_ref[1 - column]
    side = jnp.where(column == 0, others[0:1], others[2:3])
    pull = pulls[1:2] + side + arrived[0:1] + arrived[1:2]
    inner = jnp.sum(root * pull, axis=1, keepdims=True)
    mean_weight = jnp.sum(root * inner, axis=0, keepdims=True)
    transform = ((count - 1.0) ** 0.5 * root + mean_weight).astype(BF16)
    grown = jnp.dot(transform, spread_ref[column], preferred_element_type=F32)
    analysis = center_ref[column] + grown
    out_ref[:, column] = analysis.reshape(peers, held, values).astype(BF16)


def chip_body(parity_ref, *refs):
    analysis_of(1 - parity_ref[0], *refs)


def next_body(parity_ref, done_ref, *refs):
    analysis_of(parity_ref[0], *refs)


def call(body, flops, outs, *operands, aliases=None):
    return pl.pallas_call(
        body,
        out_shape=outs,
        in_specs=[
            pl.BlockSpec(memory_space=pltpu.SMEM if operand.ndim == 1 else pltpu.VMEM)
            for operand in operands
        ],
        out_specs=jax.tree.map(lambda _: pl.BlockSpec(memory_space=pltpu.VMEM), outs),
        input_output_aliases=aliases or {},
        compiler_params=pltpu.CompilerParams(vmem_limit_bytes=24 << 20),
        cost_estimate=pl.CostEstimate(flops=flops, bytes_accessed=1 << 20, transcendentals=0),
    )(*operands)


def exchange(value):
    return lax.all_to_all(
        value, "mem", split_axis=0, concat_axis=0, tiled=True, axis_index_groups=[walk()]
    )


def analyse(background, tally, slot, datum, precision, offset):
    columns, held, values = background.shape
    peers, groups = lax.axis_size("mem"), lax.axis_size("grp")
    count = peers * held
    order = walk()
    members = exchange(background).reshape(peers, 2, held, values)
    live = jnp.arange(values, dtype=jnp.int32)[None, :] < tally[:, None]
    observations = jnp.stack(
        [slot.astype(F32), datum, precision * live.astype(F32), offset], axis=0
    )
    observations = lax.ppermute(
        observations.reshape(8, values), "mem", [(p, order[p]) for p in range(peers)]
    ).reshape(4, 2, values)
    bins = jnp.stack([binned(observations[:, c], values) for c in range(2)])
    shape = jax.ShapeDtypeStruct
    sent = shape((count + 16, count), BF16)
    flops = 2 * count * count * values
    parity = (lax.axis_index("mem") % 2).astype(jnp.int32)[None]
    spread, center, pulls, to_chip, to_next = call(
        outgoing_body,
        2 * flops,
        (
            shape((2, count, values), BF16),
            shape((2, 1, values), F32),
            shape((2, 3, count), F32),
            sent,
            sent,
        ),
        parity,
        members,
        bins,
    )
    ring = [group * peers + place for group in range(groups) for place in order]
    pairs = [tuple(ring[n : n + 2]) for n in range(0, len(ring), 2)]
    gaps = [(pairs[n - 1][1], pairs[n][0]) for n in range(len(pairs))]
    from_next = lax.ppermute(to_next, BOTH, gaps + [(b, a) for a, b in gaps])
    from_chip = lax.ppermute(to_chip, BOTH, pairs + [(b, a) for a, b in pairs])
    system = call(local_body, 4 * flops, shape((2, count, count), F32), spread, bins)
    flops = flops + 10 * 3 * 2 * count**3
    out = shape((peers, 2, held, values), BF16)
    shared = (spread, center)
    partial = call(chip_body, flops, out, parity, system, pulls, from_chip, *shared)
    analysis = call(
        next_body, flops, out, parity, partial, system, pulls, from_next, *shared, aliases={1: 0}
    )
    return exchange(analysis.reshape(columns, held, values))


def solution(mesh):
    in_specs = (
        P("grp", "mem", None),
        P(BOTH),
        P(BOTH, None),
        P(BOTH, None),
        P(BOTH, None),
        P(BOTH, None),
    )
    return jax.shard_map(analyse, mesh=mesh, in_specs=in_specs, out_specs=P("grp", "mem", None), check_vma=False)
```

time: 91.2 us -> 88 us (0.965)
  starting transfers between devices: 19.6 us -> 16.3 us
  Pallas kernels: 5.85 us -> 8.75 us
  blocking collectives: 35.5 us -> 34.1 us
  waiting for transfers between devices: 25.7 us -> 24.3 us
    all_to_all x1, waiting for transfers between devices: 0.01 us -> 24.3 us  [exchange(): lax.all_to_all(value, 'mem', split_axis=0, concat_axis=0, tiled=True, axi...]
    ppermute x1, waiting for transfers between devices: 23.9 us -> 0.01 us  [analyse(): lax.ppermute(observations.reshape(8, values), 'mem', [(p, order[p]) for p...]
    pallas_call x3 -> x4, Pallas kernels: 5.85 us -> 8.75 us  [call(): pl.pallas_call(body, out_shape=outs, in_specs=[pl.BlockSpec(memory_space=...]
    ppermute x1, starting transfers between devices: 3.23 us -> 0.66 us  [analyse(): lax.ppermute(observations.reshape(8, values), 'mem', [(p, order[p]) for p...]
    ppermute x2, waiting for transfers between devices: 1.79 us -> 0.01 us  [the longest x1 0.01 us: analyse(): from_next = lax.ppermute(to_next, BOTH, gaps + [(b, a) for a, b in gaps])]
    all_to_all x1, blocking collectives: 35.5 us -> 34.1 us  [exchange(): lax.all_to_all(value, 'mem', split_axis=0, concat_axis=0, tiled=True, axi...]
  transfers between devices with their start and end apart: 4 -> 4, of which waited for: 2 -> 1; matrix products, arithmetic and copies ran while one was open for 3% -> 4% of each run, Pallas kernels for 1% -> 5%
where the time goes in v4:
time: 88 us; the launch traced here: 87.7 us
  blocking collectives  34.1 us (39%)
  waiting for transfers between devices  24.3 us (28%)
  starting transfers between devices  16.3 us (19%)
  Pallas kernels  8.75 us (10%)
  matrix products  2.93 us (3%)
  local copies, waits for them, and re-layouts  1.04 us (1%)
    all_to_all x1, blocking collectives, exchange(): lax.all_to_all(value, 'mem', split_axis=0, concat_axis=0, tiled=True, axi...  34.1 us
    all_to_all x1, waiting for transfers between devices, exchange(): lax.all_to_all(value, 'mem', split_axis=0, concat_axis=0, tiled=True, axi...  24.3 us
    all_to_all x1, starting transfers between devices, exchange(): lax.all_to_all(value, 'mem', split_axis=0, concat_axis=0, tiled=True, axi...  13.3 us
    pallas_call x4, Pallas kernels, call(): pl.pallas_call(body, out_shape=outs, in_specs=[pl.BlockSpec(memory_space=...  8.75 us
    dot_general x2, matrix products, binned(): return jnp.dot(rows, chosen, precision=HIGHEST)  2.93 us
  transfers between devices with their start and end apart: 4, of which 1 were waited for; matrix products, arithmetic and copies ran while one was open for 4% of the time, Pallas kernels for 5%

profile of v4, /device:TPU:1, one launch (start us, length us, event | category | flops | bytes accessed | tf_op | source)
XLA Modules:
  0.0 87.7 jit_solution(6194030137076012010)
XLA Ops:
  0.0 0.0 copy-start
  0.0 0.0 copy-start.1
  0.0 0.0 copy-start.4
  0.0 0.0 copy-start.2
  0.0 0.0 copy-start.3
  0.0 13.3 %all-to-all-start = ((bf16[128,4,1024]{2,1,0:T(4,128)(2,1)}), bf16[128,4,1024]{2,1,0:T(4,128)(2,1)S(1)}, u32[]{:S(2)}, u32[]{:S(2)}) async-start(bf16[128,4,1024]{2,1,0:T(4,128)(2,1)} %param.6), calls=%async_computation | async-start | bytes 2097152 | tf_op jit(solution)/shard_map/all_to_all | solution.py:167
  13.3 0.0 copy-done
  13.3 0.0 copy-done.1
  13.4 0.0 copy-done.4
  13.4 0.1 fusion.12
  13.4 0.0 copy-done.2
  13.4 0.0 copy-done.3
  13.5 0.7 collective-permute-start
  14.2 0.0 collective-permute-done
  14.2 0.1 exponential_bitcast_fusion.5
  14.3 1.5 %fusion.5 = f32[1,6,1024]{2,1,0:T(8,128)S(1)} fusion(s32[1024]{0:T(1024)S(1)} %bitcast.40, f32[3,1024]{1,0:T(4,128)S(1)} %get-tuple-element.28, f32[3,1024]{1,0:T(4,128)S(1)} %get-tuple-element.27), kind=kOutput, calls=%fused_computation.7 | convolution fusion | flops 76552192 | bytes 53248 | tf_op jit(solution)/shard_map/dot_general | solution.py:29
  15.8 1.5 %fusion.4 = f32[1,6,1024]{2,1,0:T(8,128)S(1)} fusion(s32[1024]{0:T(1024)S(1)} %bitcast.39, f32[3,1024]{1,0:T(4,128)S(1)} %get-tuple-element.31, f32[3,1024]{1,0:T(4,128)S(1)} %get-tuple-element.32), kind=kOutput, calls=%fused_computation.6 | convolution fusion | flops 76552192 | bytes 53248 | tf_op jit(solution)/shard_map/dot_general | solution.py:29
  17.3 24.3 %all-to-all-done = bf16[128,4,1024]{2,1,0:T(4,128)(2,1)S(1)} async-done(((bf16[128,4,1024]{2,1,0:T(4,128)(2,1)}), bf16[128,4,1024]{2,1,0:T(4,128)(2,1)S(1)}, u32[]{:S(2)}, u32[]{:S(2)}) %all-to-all-start) | async-done | bytes 1048608 | tf_op jit(solution)/shard_map/all_to_all | solution.py:167
  41.6 1.1 %shard_map.64 = (bf16[2,256,1024]{2,1,0:T(8,128)(2,1)S(1)}, f32[2,1,1024]{2,1,0:T(1,128)S(1)}, f32[2,3,256]{2,1,0:T(4,128)S(1)}, bf16[272,256]{1,0:T(8,128)(2,1)S(1)}, bf16[272,256]{1,0:T(8,128)(2,1)S(1)}) custom-call(s32[1]{0:T(128)} %bitcast.parity_ref, bf16[64,2,4,1024]{3,2,1,0:T(4,128)(2,1)S(1)} %bitcast.31, f32[2,6,1024]{2,1,0:T(8,128)S(1)} %pad_maximum_fusion.bins_ref), custom_call_target="tpu_custom_call" | custom-call | flops 268435456 | bytes 1048576 | tf_op jit(solution)/shard_map/pallas_call | solution.py:152
  42.6 1.2 %collective-permute-start.1 = (bf16[272,256]{1,0:T(8,128)(2,1)S(1)}, bf16[272,256]{1,0:T(8,128)(2,1)S(1)}, u32[]{:S(2)}, u32[]{:S(2)}) collective-permute-start(bf16[272,256]{1,0:T(8,128)(2,1)S(1)} %get-tuple-element.12), channel_id=1, source_target_pairs={{0,1},{2,3},{4,5},{6,7},{14,15},{12,13},{10,11},{8,9},{16,17},{18,... | collective-permute-start | bytes 417800 | tf_op jit(solution)/shard_map/ppermute | solution.py:208
  43.8 1.2 %collective-permute-start.2 = (bf16[272,256]{1,0:T(8,128)(2,1)S(1)}, bf16[272,256]{1,0:T(8,128)(2,1)S(1)}, u32[]{:S(2)}, u32[]{:S(2)}) collective-permute-start(bf16[272,256]{1,0:T(8,128)(2,1)S(1)} %get-tuple-element.14), channel_id=1, source_target_pairs={{249,0},{1,2},{3,4},{5,6},{7,14},{15,12},{13,10},{11,8},{9,16},{17... | collective-permute-start | bytes 417800 | tf_op jit(solution)/shard_map/ppermute | solution.py:207
  45.0 0.7 shard_map.65.refs_0_
  45.7 0.0 collective-permute-done.1.refs_2_
  45.7 3.5 %shard_map.66.done_ref = bf16[64,2,4,1024]{3,2,1,0:T(4,128)(2,1)S(1)} custom-call(s32[1]{0:T(128)} %bitcast.parity_ref, f32[2,256,256]{2,1,0:T(8,128)S(1)} %shard_map.65.refs_0_, f32[2,3,256]{2,1,0:T(4,128)S(1)} %get-tuple-element.11.refs_1_, bf16[272,256]{1,0:T(8,128)(2,1)S(1)} %collective-permute-done.1.refs_2_, ...), custom_call_target="tpu_custom_call" | custom-call | flops 1140850688 | bytes 1048576 | tf_op jit(solution)/shard_map/pallas_call | solution.py:152
  49.2 0.0 collective-permute-done.2.refs_2_
  49.2 3.5 %shard_map.67 = bf16[64,2,4,1024]{3,2,1,0:T(4,128)(2,1)S(1)} custom-call(s32[1]{0:T(128)} %bitcast.parity_ref, bf16[64,2,4,1024]{3,2,1,0:T(4,128)(2,1)S(1)} %shard_map.66.done_ref, f32[2,256,256]{2,1,0:T(8,128)S(1)} %shard_map.65.refs_0_, f32[2,3,256]{2,1,0:T(4,128)S(1)} %get-tuple-element.11.refs_1_, ...), custom_call_target="tpu_custom_call", output_to_operand_aliasing={{}: (1, {})} | custom-call | flops 1140850688 | bytes 1048576 | tf_op jit(solution)/shard_map/pallas_call | solution.py:152
  52.7 34.1 %all_to_all.10 = bf16[128,4,1024]{2,1,0:T(4,128)(2,1)S(1)} all-to-all(bf16[128,4,1024]{2,1,0:T(4,128)(2,1)S(1)} %bitcast.32), channel_id=1, replica_groups={{0,1,2,3,4,5,6,7,14,15,12,13,10,11,8,9,16,17,18,19,20,21,22,23,30,31,28..., dimensions={0} | all-to-all | bytes 2097152 | tf_op jit(solution)/shard_map/all_to_all | solution.py:167
  86.8 1.0 %copy.10 = bf16[128,4,1024]{2,1,0:T(4,128)(2,1)} copy(bf16[128,4,1024]{2,1,0:T(4,128)(2,1)S(1)} %all_to_all.10) | data formatting | bytes 2097152
  (6 shorter events, 0.1 us)
Async XLA Ops:
  0.0 13.3 %copy-start = (s32[2,1024]{1,0:T(2,128)S(1)}, s32[2,1024]{1,0:T(2,128)}, u32[]{:S(2)}) copy-start(s32[2,1024]{1,0:T(2,128)} %param.8) | copy-start | bytes 24580
  0.0 13.3 %copy-start.1 = (f32[2,1024]{1,0:T(2,128)S(1)}, f32[2,1024]{1,0:T(2,128)}, u32[]{:S(2)}) copy-start(f32[2,1024]{1,0:T(2,128)} %param.10) | copy-start | bytes 24580
  0.0 13.4 %copy-start.4 = (s32[2]{0:T(128)S(1)}, s32[2]{0:T(128)}, u32[]{:S(2)}) copy-start(s32[2]{0:T(128)} %param.7) | copy-start | bytes 28
  0.0 13.4 %copy-start.2 = (f32[2,1024]{1,0:T(2,128)S(1)}, f32[2,1024]{1,0:T(2,128)}, u32[]{:S(2)}) copy-start(f32[2,1024]{1,0:T(2,128)} %param.11) | copy-start | bytes 24580
  0.0 13.4 %copy-start.3 = (f32[2,1024]{1,0:T(2,128)S(1)}, f32[2,1024]{1,0:T(2,128)}, u32[]{:S(2)}) copy-start(f32[2,1024]{1,0:T(2,128)} %param.9) | copy-start | bytes 24580
  0.0 41.5 %all-to-all-start = ((bf16[128,4,1024]{2,1,0:T(4,128)(2,1)}), bf16[128,4,1024]{2,1,0:T(4,128)(2,1)S(1)}, u32[]{:S(2)}, u32[]{:S(2)}) async-start(bf16[128,4,1024]{2,1,0:T(4,128)(2,1)} %param.6), calls=%async_computation | async-start | bytes 2097152 | tf_op jit(solution)/shard_map/all_to_all | solution.py:167
  13.5 0.7 collective-permute-start
  42.6 3.1 %collective-permute-start.1 = (bf16[272,256]{1,0:T(8,128)(2,1)S(1)}, bf16[272,256]{1,0:T(8,128)(2,1)S(1)}, u32[]{:S(2)}, u32[]{:S(2)}) collective-permute-start(bf16[272,256]{1,0:T(8,128)(2,1)S(1)} %get-tuple-element.12), channel_id=1, source_target_pairs={{0,1},{2,3},{4,5},{6,7},{14,15},{12,13},{10,11},{8,9},{16,17},{18,... | collective-permute-start | bytes 417800 | tf_op jit(solution)/shard_map/ppermute | solution.py:208
  43.8 5.4 %collective-permute-start.2 = (bf16[272,256]{1,0:T(8,128)(2,1)S(1)}, bf16[272,256]{1,0:T(8,128)(2,1)S(1)}, u32[]{:S(2)}, u32[]{:S(2)}) collective-permute-start(bf16[272,256]{1,0:T(8,128)(2,1)S(1)} %get-tuple-element.14), channel_id=1, source_target_pairs={{249,0},{1,2},{3,4},{5,6},{7,14},{15,12},{13,10},{11,8},{9,16},{17... | collective-permute-start | bytes 417800 | tf_op jit(solution)/shard_map/ppermute | solution.py:207

commit v5 on v4

--- a/solution.py
+++ b/solution.py
@@ -46,10 +46,12 @@
 
 def product(left, right):
     (left_high, left_low), (right_high, right_low) = left, right
-    return jnp.dot(
-        jnp.concatenate([left_high, left_high, left_low], axis=1),
-        jnp.concatenate([right_high, right_low, right_high], axis=0),
-        preferred_element_type=F32,
+    rows = jnp.concatenate([left_high, left_high, left_low], axis=1)
+    stacked = jnp.concatenate([right_high, right_low, right_high], axis=0)
+    middle = rows.shape[0] // 2
+    return jnp.concatenate(
+        [jnp.dot(part, stacked, preferred_element_type=F32) for part in (rows[:middle], rows[middle:])],
+        axis=0,
     )
 
 
@@ -57,48 +59,42 @@
     return lax.dot_general(left, right, (((1,), (1,)), ((), ())), preferred_element_type=F32)
 
 
-def rows_of(spread, bins, which):
-    return (spread.astype(F32) * jnp.sqrt(bins[which : which + 1])).astype(BF16)
-
-
-def pulls_of(spread, center, bins):
-    high, low = halves(bins[3:6] - bins[0:3] * center)
-    both = against(jnp.concatenate([high, low], axis=0), spread)
-    return both[0:3] + both[3:6]
-
-
-def outgoing_body(
-    parity_ref, members_ref, bins_ref, spread_ref, center_ref, pulls_ref, chip_ref, next_ref
-):
+def weighed(spread, center, weight, driven):
+    high, low = halves(driven - weight * center)
+    rows = (spread.astype(F32) * weight).astype(BF16)
+    return jnp.concatenate([rows, high, low, jnp.zeros((14, rows.shape[1]), BF16)], axis=0)
+
+
+def outgoing_body(parity_ref, members_ref, bins_ref, spread_ref, center_ref, chip_ref, next_ref):
     peers, _, held, values = members_ref.shape
     count = peers * held
     for column in (0, 1):
         wide = members_ref[:, column].astype(F32).reshape(count, values)
         center = jnp.sum(wide, axis=0, keepdims=True) * (1.0 / count)
         center_ref[column] = center
-        spread = (wide - center).astype(BF16)
-        spread_ref[column] = spread
-        pulls_ref[column] = pulls_of(spread, center, bins_ref[column])
+        spread_ref[column] = (wide - center).astype(BF16)
     parity = parity_ref[0]
     for column, sent in ((parity, next_ref), (1 - parity, chip_ref)):
-        even = column == 0
-        bins, pulls = bins_ref[column], pulls_ref[column]
-        scale = jnp.sqrt(jnp.where(even, bins[0:1], bins[2:3]))
-        rows = (spread_ref[column].astype(F32) * scale).astype(BF16)
-        sent[0:count, :] = against(rows, rows).astype(BF16)
-        high, low = halves(jnp.where(even, pulls[0:1], pulls[2:3]))
+        bins, spread = bins_ref[column], spread_ref[column]
+        weight = jnp.where(column == 0, bins[0:1], bins[2:3])
+        driven = jnp.where(column == 0, bins[3:4], bins[5:6])
+        gram = against(weighed(spread, center_ref[column], weight, driven), spread)
+        sent[0:count, :] = gram[0:count].astype(BF16)
+        high, low = halves(gram[count : count + 1] + gram[count + 1 : count + 2])
         sent[count:, :] = jnp.concatenate([high, low, jnp.zeros((14, count), BF16)], axis=0)
 
 
-def local_body(spread_ref, bins_ref, system_ref):
+def local_body(spread_ref, center_ref, bins_ref, local_ref):
     for column, other, which in ((0, 1, 0), (1, 0, 2)):
-        own = rows_of(spread_ref[column], bins_ref[column], 1)
-        side = rows_of(spread_ref[other], bins_ref[other], which)
-        rows = jnp.concatenate([own, side], axis=1)
-        system_ref[column] = against(rows, rows)
-
-
-def analysis_of(column, system_ref, pulls_ref, received_ref, spread_ref, center_ref, out_ref):
+        left = [
+            weighed(spread_ref[c], center_ref[c], bins_ref[c, w : w + 1], bins_ref[c, 3 + w : 4 + w])
+            for c, w in ((column, 1), (other, which))
+        ]
+        right = [spread_ref[column], spread_ref[other]]
+        local_ref[column] = against(jnp.concatenate(left, axis=1), jnp.concatenate(right, axis=1))
+
+
+def analysis_of(column, local_ref, received_ref, spread_ref, center_ref, out_ref):
     peers, _, held, values = out_ref.shape
     count = peers * held
     diagonal = lax.broadcasted_iota(jnp.int32, (count, count), 0) == lax.broadcasted_iota(
@@ -108,30 +104,32 @@
     def scaled_eye(value):
         return jnp.where(diagonal, value, 0.0).astype(F32)
 
-    def two_steps(ratio):
-        split = halves(ratio)
-        square = 0.25 * product(split, split)
+    def two_steps(square, value):
         factors = [
-            halves(square + linear * ratio + scaled_eye(constant))
+            halves(square + linear * value + scaled_eye(constant))
             for linear, constant in two_step_factors()
         ]
-        return split, halves(product(*factors))
-
-    def advanced(split, gain):
-        return product(split, halves(product(gain, gain)))
-
-    system = scaled_eye(count - 1.0) + system_ref[column] + received_ref[0:count, :].astype(F32)
-    squares = jnp.sum(jnp.sum(system * system, axis=0, keepdims=True), axis=1, keepdims=True)
+        return halves(product(*factors))
+
+    def stacked(*values):
+        return tuple(jnp.concatenate(parts, axis=0) for parts in zip(*values))
+
+    combined = local_ref[column] + received_ref[...].astype(F32)
+    system = scaled_eye(count - 1.0) + combined[0:count]
+    whole = halves(system)
+    squares = jnp.sum(jnp.sum((system * system).reshape(count // 8, 8, count), axis=0), axis=(0, 1), keepdims=True)
     norm = jnp.sqrt(squares)
-    split, first = two_steps(system * (1.0 / norm))
-    split, second = two_steps(advanced(split, first))
-    inverse = halves(product(first, second))
-    last = halves(scaled_eye(1.5) - 0.5 * advanced(split, second))
-    root = product(last, inverse) * (1.0 / jnp.sqrt(norm))
-    arrived = received_ref[count:, :].astype(F32)
-    pulls, others = pulls_ref[column], pulls_ref[1 - column]
-    side = jnp.where(column == 0, others[0:1], others[2:3])
-    pull = pulls[1:2] + side + arrived[0:1] + arrived[1:2]
+    scale = 1.0 / norm
+    first = two_steps(product(whole, whole) * (0.25 * scale * scale), system * scale)
+    value = product(whole, halves(product(first, first))) * scale
+    later = halves(value)
+    both = product(stacked(later, first), later)
+    second = two_steps(0.25 * both[:count], value)
+    three = product(stacked(second, first, halves(both[count:])), second)
+    twice, inverse, carried = three[:count], three[count : 2 * count], three[2 * count :]
+    root = 1.5 * inverse - 0.5 * product(halves(carried), halves(twice))
+    root = root * (1.0 / jnp.sqrt(norm))
+    pull = combined[count : count + 1] + combined[count + 1 : count + 2]
     inner = jnp.sum(root * pull, axis=1, keepdims=True)
     mean_weight = jnp.sum(root * inner, axis=0, keepdims=True)
     transform = ((count - 1.0) ** 0.5 * root + mean_weight).astype(BF16)
@@ -187,13 +185,12 @@
     sent = shape((count + 16, count), BF16)
     flops = 2 * count * count * values
     parity = (lax.axis_index("mem") % 2).astype(jnp.int32)[None]
-    spread, center, pulls, to_chip, to_next = call(
+    spread, center, to_chip, to_next = call(
         outgoing_body,
         2 * flops,
         (
             shape((2, count, values), BF16),
             shape((2, 1, values), F32),
-            shape((2, 3, count), F32),
             sent,
             sent,
         ),
@@ -206,13 +203,15 @@
     gaps = [(pairs[n - 1][1], pairs[n][0]) for n in range(len(pairs))]
     from_next = lax.ppermute(to_next, BOTH, gaps + [(b, a) for a, b in gaps])
     from_chip = lax.ppermute(to_chip, BOTH, pairs + [(b, a) for a, b in pairs])
-    system = call(local_body, 4 * flops, shape((2, count, count), F32), spread, bins)
+    local = call(
+        local_body, 4 * flops, shape((2, count + 16, count), F32), spread, center, bins
+    )
     flops = flops + 10 * 3 * 2 * count**3
     out = shape((peers, 2, held, values), BF16)
     shared = (spread, center)
-    partial = call(chip_body, flops, out, parity, system, pulls, from_chip, *shared)
+    partial = call(chip_body, flops, out, parity, local, from_chip, *shared)
     analysis = call(
-        next_body, flops, out, parity, partial, system, pulls, from_next, *shared, aliases={1: 0}
+        next_body, flops, out, parity, partial, local, from_next, *shared, aliases={1: 0}
     )
     return exchange(analysis.reshape(columns, held, values))
 

time: 88 us -> 87.3 us (level)
  Pallas kernels: 8.75 us -> 7.48 us
    pallas_call x4, Pallas kernels: 8.75 us -> 7.48 us  [call(): pl.pallas_call(body, out_shape=outs, in_specs=[pl.BlockSpec(memory_space=...]
  transfers between devices with their start and end apart: 4 -> 4, of which waited for: 1 -> 1; matrix products, arithmetic and copies ran while one was open for 4% -> 4% of each run, Pallas kernels for 5% -> 4%
where the time goes in v5:
time: 87.3 us; the launch traced here: 87.1 us
  blocking collectives  34.7 us (40%)
  waiting for transfers between devices  24.3 us (28%)
  starting transfers between devices  16.3 us (19%)
  Pallas kernels  7.48 us (9%)
  matrix products  2.93 us (3%)
  local copies, waits for them, and re-layouts  1.04 us (1%)
    all_to_all x1, blocking collectives, exchange(): lax.all_to_all(value, 'mem', split_axis=0, concat_axis=0, tiled=True, axi...  34.7 us
    all_to_all x1, waiting for transfers between devices, exchange(): lax.all_to_all(value, 'mem', split_axis=0, concat_axis=0, tiled=True, axi...  24.3 us
    all_to_all x1, starting transfers between devices, exchange(): lax.all_to_all(value, 'mem', split_axis=0, concat_axis=0, tiled=True, axi...  13.3 us
    pallas_call x4, Pallas kernels, call(): pl.pallas_call(body, out_shape=outs, in_specs=[pl.BlockSpec(memory_space=...  7.48 us
    dot_general x2, matrix products, binned(): return jnp.dot(rows, chosen, precision=HIGHEST)  2.93 us
  transfers between devices with their start and end apart: 4, of which 1 were waited for; matrix products, arithmetic and copies ran while one was open for 4% of the time, Pallas kernels for 4%

profile of v5, /device:TPU:1, one launch (start us, length us, event | category | flops | bytes accessed | tf_op | source)
XLA Modules:
  0.0 87.1 jit_solution(17109442741535082539)
XLA Ops:
  0.0 0.0 copy-start
  0.0 0.0 copy-start.1
  0.0 0.0 copy-start.4
  0.0 0.0 copy-start.2
  0.0 0.0 copy-start.3
  0.0 13.3 %all-to-all-start = ((bf16[128,4,1024]{2,1,0:T(4,128)(2,1)}), bf16[128,4,1024]{2,1,0:T(4,128)(2,1)S(1)}, u32[]{:S(2)}, u32[]{:S(2)}) async-start(bf16[128,4,1024]{2,1,0:T(4,128)(2,1)} %param.6), calls=%async_computation | async-start | bytes 2097152 | tf_op jit(solution)/shard_map/all_to_all | solution.py:165
  13.3 0.0 copy-done
  13.3 0.0 copy-done.1
  13.4 0.0 copy-done.4
  13.4 0.1 fusion.12
  13.4 0.0 copy-done.2
  13.4 0.0 copy-done.3
  13.5 0.7 collective-permute-start
  14.2 0.0 collective-permute-done
  14.2 0.1 exponential_bitcast_fusion.5
  14.3 1.5 %fusion.5 = f32[1,6,1024]{2,1,0:T(8,128)S(1)} fusion(s32[1024]{0:T(1024)S(1)} %bitcast.40, f32[3,1024]{1,0:T(4,128)S(1)} %get-tuple-element.26, f32[3,1024]{1,0:T(4,128)S(1)} %get-tuple-element.25), kind=kOutput, calls=%fused_computation.7 | convolution fusion | flops 76552192 | bytes 53248 | tf_op jit(solution)/shard_map/dot_general | solution.py:29
  15.8 1.5 %fusion.4 = f32[1,6,1024]{2,1,0:T(8,128)S(1)} fusion(s32[1024]{0:T(1024)S(1)} %bitcast.39, f32[3,1024]{1,0:T(4,128)S(1)} %get-tuple-element.29, f32[3,1024]{1,0:T(4,128)S(1)} %get-tuple-element.30), kind=kOutput, calls=%fused_computation.6 | convolution fusion | flops 76552192 | bytes 53248 | tf_op jit(solution)/shard_map/dot_general | solution.py:29
  17.3 24.3 %all-to-all-done = bf16[128,4,1024]{2,1,0:T(4,128)(2,1)S(1)} async-done(((bf16[128,4,1024]{2,1,0:T(4,128)(2,1)}), bf16[128,4,1024]{2,1,0:T(4,128)(2,1)S(1)}, u32[]{:S(2)}, u32[]{:S(2)}) %all-to-all-start) | async-done | bytes 1048608 | tf_op jit(solution)/shard_map/all_to_all | solution.py:165
  41.6 1.0 %shard_map.64 = (bf16[2,256,1024]{2,1,0:T(8,128)(2,1)S(1)}, f32[2,1,1024]{2,1,0:T(1,128)S(1)}, bf16[272,256]{1,0:T(8,128)(2,1)S(1)}, bf16[272,256]{1,0:T(8,128)(2,1)S(1)}) custom-call(s32[1]{0:T(128)} %bitcast.parity_ref, bf16[64,2,4,1024]{3,2,1,0:T(4,128)(2,1)S(1)} %bitcast.31, f32[2,6,1024]{2,1,0:T(8,128)S(1)} %pad_maximum_fusion.bins_ref), custom_call_target="tpu_custom_call" | custom-call | flops 268435456 | bytes 1048576 | tf_op jit(solution)/shard_map/pallas_call | solution.py:150
  42.6 1.2 %collective-permute-start.1 = (bf16[272,256]{1,0:T(8,128)(2,1)S(1)}, bf16[272,256]{1,0:T(8,128)(2,1)S(1)}, u32[]{:S(2)}, u32[]{:S(2)}) collective-permute-start(bf16[272,256]{1,0:T(8,128)(2,1)S(1)} %get-tuple-element.11), channel_id=1, source_target_pairs={{0,1},{2,3},{4,5},{6,7},{14,15},{12,13},{10,11},{8,9},{16,17},{18,... | collective-permute-start | bytes 417800 | tf_op jit(solution)/shard_map/ppermute | solution.py:205
  43.8 1.2 %collective-permute-start.2 = (bf16[272,256]{1,0:T(8,128)(2,1)S(1)}, bf16[272,256]{1,0:T(8,128)(2,1)S(1)}, u32[]{:S(2)}, u32[]{:S(2)}) collective-permute-start(bf16[272,256]{1,0:T(8,128)(2,1)S(1)} %get-tuple-element.12), channel_id=1, source_target_pairs={{249,0},{1,2},{3,4},{5,6},{7,14},{15,12},{13,10},{11,8},{9,16},{17... | collective-permute-start | bytes 417800 | tf_op jit(solution)/shard_map/ppermute | solution.py:204
  44.9 0.8 shard_map.65.refs_0_
  45.7 0.0 collective-permute-done.1.refs_1_
  45.7 2.9 %shard_map.66.done_ref = bf16[64,2,4,1024]{3,2,1,0:T(4,128)(2,1)S(1)} custom-call(s32[1]{0:T(128)} %bitcast.parity_ref, f32[2,272,256]{2,1,0:T(8,128)S(1)} %shard_map.65.refs_0_, bf16[272,256]{1,0:T(8,128)(2,1)S(1)} %collective-permute-done.1.refs_1_, bf16[2,256,1024]{2,1,0:T(8,128)(2,1)S(1)} %get-tuple-element.9.spread_ref.refs_2_, ...), custom_call_target="tpu_custom_call" | custom-call | flops 1140850688 | bytes 1048576 | tf_op jit(solution)/shard_map/pallas_call | solution.py:150
  48.6 0.0 collective-permute-done.2.refs_1_
  48.6 2.8 %shard_map.67 = bf16[64,2,4,1024]{3,2,1,0:T(4,128)(2,1)S(1)} custom-call(s32[1]{0:T(128)} %bitcast.parity_ref, bf16[64,2,4,1024]{3,2,1,0:T(4,128)(2,1)S(1)} %shard_map.66.done_ref, f32[2,272,256]{2,1,0:T(8,128)S(1)} %shard_map.65.refs_0_, bf16[272,256]{1,0:T(8,128)(2,1)S(1)} %collective-permute-done.2.refs_1_, ...), custom_call_target="tpu_custom_call", output_to_operand_aliasing={{}: (1, {})} | custom-call | flops 1140850688 | bytes 1048576 | tf_op jit(solution)/shard_map/pallas_call | solution.py:150
  51.4 34.7 %all_to_all.10 = bf16[128,4,1024]{2,1,0:T(4,128)(2,1)S(1)} all-to-all(bf16[128,4,1024]{2,1,0:T(4,128)(2,1)S(1)} %bitcast.32), channel_id=1, replica_groups={{0,1,2,3,4,5,6,7,14,15,12,13,10,11,8,9,16,17,18,19,20,21,22,23,30,31,28..., dimensions={0} | all-to-all | bytes 2097152 | tf_op jit(solution)/shard_map/all_to_all | solution.py:165
  86.1 1.0 %copy.10 = bf16[128,4,1024]{2,1,0:T(4,128)(2,1)} copy(bf16[128,4,1024]{2,1,0:T(4,128)(2,1)S(1)} %all_to_all.10) | data formatting | bytes 2097152
  (6 shorter events, 0.1 us)
Async XLA Ops:
  0.0 13.3 %copy-start = (s32[2,1024]{1,0:T(2,128)S(1)}, s32[2,1024]{1,0:T(2,128)}, u32[]{:S(2)}) copy-start(s32[2,1024]{1,0:T(2,128)} %param.8) | copy-start | bytes 24580
  0.0 13.3 %copy-start.1 = (f32[2,1024]{1,0:T(2,128)S(1)}, f32[2,1024]{1,0:T(2,128)}, u32[]{:S(2)}) copy-start(f32[2,1024]{1,0:T(2,128)} %param.10) | copy-start | bytes 24580
  0.0 13.4 %copy-start.4 = (s32[2]{0:T(128)S(1)}, s32[2]{0:T(128)}, u32[]{:S(2)}) copy-start(s32[2]{0:T(128)} %param.7) | copy-start | bytes 28
  0.0 13.4 %copy-start.2 = (f32[2,1024]{1,0:T(2,128)S(1)}, f32[2,1024]{1,0:T(2,128)}, u32[]{:S(2)}) copy-start(f32[2,1024]{1,0:T(2,128)} %param.11) | copy-start | bytes 24580
  0.0 13.4 %copy-start.3 = (f32[2,1024]{1,0:T(2,128)S(1)}, f32[2,1024]{1,0:T(2,128)}, u32[]{:S(2)}) copy-start(f32[2,1024]{1,0:T(2,128)} %param.9) | copy-start | bytes 24580
  0.0 41.5 %all-to-all-start = ((bf16[128,4,1024]{2,1,0:T(4,128)(2,1)}), bf16[128,4,1024]{2,1,0:T(4,128)(2,1)S(1)}, u32[]{:S(2)}, u32[]{:S(2)}) async-start(bf16[128,4,1024]{2,1,0:T(4,128)(2,1)} %param.6), calls=%async_computation | async-start | bytes 2097152 | tf_op jit(solution)/shard_map/all_to_all | solution.py:165
  13.5 0.7 collective-permute-start
  42.6 3.1 %collective-permute-start.1 = (bf16[272,256]{1,0:T(8,128)(2,1)S(1)}, bf16[272,256]{1,0:T(8,128)(2,1)S(1)}, u32[]{:S(2)}, u32[]{:S(2)}) collective-permute-start(bf16[272,256]{1,0:T(8,128)(2,1)S(1)} %get-tuple-element.11), channel_id=1, source_target_pairs={{0,1},{2,3},{4,5},{6,7},{14,15},{12,13},{10,11},{8,9},{16,17},{18,... | collective-permute-start | bytes 417800 | tf_op jit(solution)/shard_map/ppermute | solution.py:205
  43.8 4.8 %collective-permute-start.2 = (bf16[272,256]{1,0:T(8,128)(2,1)S(1)}, bf16[272,256]{1,0:T(8,128)(2,1)S(1)}, u32[]{:S(2)}, u32[]{:S(2)}) collective-permute-start(bf16[272,256]{1,0:T(8,128)(2,1)S(1)} %get-tuple-element.12), channel_id=1, source_target_pairs={{249,0},{1,2},{3,4},{5,6},{7,14},{15,12},{13,10},{11,8},{9,16},{17... | collective-permute-start | bytes 417800 | tf_op jit(solution)/shard_map/ppermute | solution.py:204
